TPU v7x, 256 devices: a whole 4x4x8 slice. The times are simulated.
256 devices in a mesh: dp: 8 (over y, core), seq: 32 (over x, z).
Axes of the slice: x: 4, y: 4, z: 8, core: 2. Of those that a mesh axis runs over, the one named last changes fastest.
Arguments:
- means: bfloat16 [2048, 384, 192], P('dp', 'seq'), may hold values from -6 to 6
- log_scales: bfloat16 [2048, 384, 192], P('dp', 'seq'), may hold values from -0.5 to 0.5
- latents: bfloat16 [2048, 1536, 192], P('dp', 'seq'), may hold values from -7 to 7
- text_lens: int32 [2048], P('dp'), may hold values from 96 to 384
- frame_lens: int32 [2048], P('dp'), may hold values from 384 to 1536
Outputs:
- positions: float32 [2048, 1536], P('dp', 'seq')
- loss: float32 [], replicated
Inputs may be any that keep to these rules, and one draw needn't show every extreme that they name: `frame_lens`: each utterance has at least as many frames as any text can have tokens.
All inputs are finite; a program needn't handle non-finite values.
Results may differ from a plain program's by a relative error of at most 0.0065.
Values may be sent and summed in bfloat16 or wider, within the bound.
No kernel may reach another device: no remote copies, remote signals or barrier semaphores. Data moves between devices by JAX's collectives and lax.ppermute only.
A program may use at most 128 MiB of HBM per device.

v0:
```python
import functools

import jax
import jax.numpy as jnp
from jax import lax
from jax.sharding import Mesh
from jax.sharding import PartitionSpec as P

BLK = 512
SEQ = ("seq_0", "seq_1")
DP_SEQ = ("dp_0", "dp_1", "seq_0", "seq_1")
DP = ("dp_0", "dp_1")


HALF_LOG_TWO_PI = 0.9189385332046727
NEG_FILL = -1000000000.0
PAIR_DIMS = (((2,), (2,)), ((0,), (0,)))


def in_one_piece(arrays, axis, split_dim, concat_dim, along):
    ends, at = ([], 0)
    for a in arrays[:-1]:
        at += a.shape[along]
        ends.append(at)
    both = jnp.concatenate(arrays, axis=along)
    return tuple(
        jnp.split(
            lax.all_to_all(both, axis, split_axis=split_dim, concat_axis=concat_dim, tiled=True),
            ends,
            axis=along,
        )
    )


def over_axes(shard, axes):
    return functools.reduce(lax.psum, axes, shard)


def prior_terms(means, log_scales):
    mean_wide = means.astype(jnp.float32)
    scale_wide = log_scales.astype(jnp.float32)
    precision = jnp.exp(-2.0 * scale_wide)
    weighted = (mean_wide * precision).astype(jnp.bfloat16)
    prec_low = precision.astype(jnp.bfloat16)
    channels = means.shape[-1]
    offset = (
        0.5 * jnp.sum(mean_wide * mean_wide * precision, axis=-1) + jnp.sum(scale_wide, axis=-1)
    ) / channels + HALF_LOG_TWO_PI
    return (weighted, prec_low, offset)


def block_loglik(latent_block, weighted, prec_low, offset):
    latent_broadened = latent_block.astype(jnp.float32)
    squared_latent = (latent_broadened * latent_broadened).astype(jnp.bfloat16)
    cross_product_term = lax.dot_general(
        latent_block, weighted, PAIR_DIMS, preferred_element_type=jnp.float32
    )
    quadratic_term = lax.dot_general(
        squared_latent, prec_low, PAIR_DIMS, preferred_element_type=jnp.float32
    )
    return (cross_product_term - 0.5 * quadratic_term) / latent_block.shape[-1] - offset[:, None, :]


def align(latents, weighted, prec_low, offset, text_len, frame_len, block_count):
    batch = latents.shape[0]
    frames = latents.shape[1]
    tokens = weighted.shape[1]
    token_ids = jnp.arange(tokens, dtype=jnp.int32)
    block_offsets = jnp.arange(BLK, dtype=jnp.int32)
    initial = jnp.broadcast_to(
        jnp.where(token_ids == 0, 0.0, NEG_FILL).astype(jnp.float32), (batch, tokens)
    )
    token_wide = token_ids.astype(jnp.float32)
    denominator = (text_len - 1).astype(jnp.float32)

    def one_block(block_index, carried):
        previous, finish, positions = carried
        leading_frame = block_index * BLK
        latent_block = lax.dynamic_slice_in_dim(latents, leading_frame, BLK, 1)
        loglik = block_loglik(latent_block, weighted, prec_low, offset)
        frame_now = leading_frame + block_offsets
        lower = text_len[:, None, None] - frame_len[:, None, None] + frame_now[None, :, None]
        allowed = (
            (token_ids[None, None, :] < text_len[:, None, None])
            & (frame_now[None, :, None] < frame_len[:, None, None])
            & (token_ids[None, None, :] <= frame_now[None, :, None])
            & (token_ids[None, None, :] >= lower)
        )

        def one_frame(before, inputs_now):
            frame_like, allowed_now = inputs_now
            shifted = jnp.concatenate(
                [jnp.full((batch, 1), NEG_FILL, before.dtype), before[:, :-1]], axis=1
            )
            scores = jnp.where(allowed_now, frame_like + jnp.maximum(before, shifted), NEG_FILL)
            return (scores, scores)

        previous, block_scores = lax.scan(
            one_frame,
            previous,
            (jnp.moveaxis(loglik, 1, 0), jnp.moveaxis(allowed, 1, 0)),
            unroll=16,
        )
        summit = jnp.max(block_scores, axis=2, keepdims=True)
        weight = jnp.exp(block_scores - summit)
        centre = jnp.sum(weight * token_wide[None, None, :], axis=2) / jnp.sum(weight, axis=2)
        live = frame_now[:, None] < frame_len[None, :]
        frame_row = jnp.where(live, centre / denominator[None, :], 0.0)
        closing_value = (token_ids[None, None, :] == text_len[None, :, None] - 1) & (
            frame_now[:, None, None] == frame_len[None, :, None] - 1
        )
        gained = jnp.sum(jnp.where(closing_value, block_scores, 0.0), axis=(0, 2))
        positions = lax.dynamic_update_slice_in_dim(
            positions, jnp.transpose(frame_row), leading_frame, 1
        )
        return (previous, finish + gained, positions)

    carried = (initial, jnp.zeros((batch,), jnp.float32), jnp.zeros((batch, frames), jnp.float32))
    carried = lax.fori_loop(0, block_count, one_block, carried)
    return (carried[2], carried[1])


def shards(means, log_scales, latents, text_lens, frame_lens):
    owners = lax.axis_size(SEQ)
    group_size = frame_lens.shape[0]
    per_owner = group_size // owners
    own_start = lax.axis_index(SEQ) * per_owner
    text_own = lax.dynamic_slice_in_dim(text_lens, own_start, per_owner)
    frame_own = lax.dynamic_slice_in_dim(frame_lens, own_start, per_owner)
    means, log_scales, latents = (
        *in_one_piece((means, log_scales), SEQ, 0, 1, 2),
        lax.all_to_all(latents, SEQ, split_axis=0, concat_axis=1, tiled=True),
    )
    weighted, prec_low, offset = prior_terms(means, log_scales)
    frames = latents.shape[1]
    positions, finish = align(
        latents, weighted, prec_low, offset, text_own, frame_own, frames // BLK
    )
    positions = lax.all_to_all(positions, SEQ, split_axis=1, concat_axis=0, tiled=True)
    path_total, frame_total = (
        over_axes(jnp.sum(finish), DP_SEQ),
        over_axes(jnp.sum(frame_own).astype(jnp.float32), DP_SEQ),
    )
    return (positions, -path_total / frame_total)


def solution(mesh):
    torus = Mesh(mesh.devices.reshape(4, 2, 4, 8), ("dp_0", "dp_1", "seq_0", "seq_1"))
    in_specs = (P(DP, SEQ, None), P(DP, SEQ, None), P(DP, SEQ, None), P(DP), P(DP))
    out_specs = (P(DP, SEQ), P())
    return jax.shard_map(
        shards, mesh=torus, in_specs=in_specs, out_specs=out_specs, check_vma=False
    )
```

profile of v0, /device:TPU:32, one launch (start us, length us, event | category | flops | bytes accessed | tf_op | source)
XLA Modules:
  0.0 783.1 jit_solution(6653686788013678887)
XLA Ops:
  7.3 4.5 pad_maximum_fusion
  11.8 11.2 %all-to-all-start.1 = ((bf16[256,12,384]{2,1,0:T(8,128)(2,1)}), bf16[256,12,384]{2,1,0:T(8,128)(2,1)S(1)}, u32[]{:S(2)}, u32[]{:S(2)}) async-start(bf16[256,12,384]{2,1,0:T(8,128)(2,1)} %pad_maximum_fusion), calls=%async_computation.1 | async-start | bytes 6291456 | tf_op jit(solution)/shard_map/all_to_all | solution.py:28
  23.0 9.1 %copy.42 = bf16[256,48,192]{2,1,0:T(8,128)(2,1)} copy(bf16[256,48,192]{0,2,1:T(8,128)(2,1)} %param.11) | data formatting | bytes 9437184 | tf_op args[2]
  32.0 61.9 %all-to-all-done.1 = bf16[256,12,384]{2,1,0:T(8,128)(2,1)S(1)} async-done(((bf16[256,12,384]{2,1,0:T(8,128)(2,1)}), bf16[256,12,384]{2,1,0:T(8,128)(2,1)S(1)}, u32[]{:S(2)}, u32[]{:S(2)}) %all-to-all-start.1) | async-done | bytes 2359328 | tf_op jit(solution)/shard_map/all_to_all | solution.py:28
  94.0 9.6 %all-to-all-start = ((bf16[256,48,192]{2,1,0:T(8,128)(2,1)}), bf16[256,48,192]{2,1,0:T(8,128)(2,1)}, u32[]{:S(2)}, u32[]{:S(2)}) async-start(bf16[256,48,192]{2,1,0:T(8,128)(2,1)} %copy.42), calls=%async_computation | async-start | bytes 12582912 | tf_op jit(solution)/shard_map/all_to_all | solution.py:132
  111.2 132.9 %all-to-all-done = bf16[256,48,192]{2,1,0:T(8,128)(2,1)} async-done(((bf16[256,48,192]{2,1,0:T(8,128)(2,1)}), bf16[256,48,192]{2,1,0:T(8,128)(2,1)}, u32[]{:S(2)}, u32[]{:S(2)}) %all-to-all-start) | async-done | bytes 4718624 | tf_op jit(solution)/shard_map/all_to_all | solution.py:132
  244.0 6.1 copy.43
  250.1 8.0 %copy.50 = bf16[8,1536,192]{1,2,0:T(8,128)(2,1)} copy(bf16[8,1536,192]{2,1,0:T(8,128)(2,1)} %bitcast.381) | data formatting | bytes 9437184
  258.0 468.9 %while.66 = (s32[]{:T(128)}, f32[8,384]{1,0:T(8,128)S(1)}, f32[8]{0:T(128)S(1)}, f32[8,1536]{1,0:T(8,128)S(1)}, bf16[8,1536,192]{1,2,0:T(8,128)(2,1)}, /*index=5...) while((s32[]{:T(128)}, f32[8,384]{1,0:T(8,128)S(1)}, ...), condition=%wide.region_9.10_spmd.clone.clone.clone, body=%wide.region_2.9_spmd.clone.clone.sunk.clone | while | flops 1234287872 | bytes 50425856 | solution.py:119
  261.5 5.5 multiply_subtract_fusion.3
  269.9 133.0 %while.65 = (s32[]{:T(128)}, f32[8,384]{1,0:T(8,128)S(1)}, f32[32,16,8,384]{3,2,1,0:T(8,128)}, pred[32,16,8,384]{3,2,1,0:T(8,128)(4,1)S(1)}, f32[32,16,8,384]{3,...) while((s32[]{:T(128)}, f32[8,384]{1,0:T(8,128)S(1)}, ...), condition=%wide.region_4.4_spmd, body=%wide.region_3.3_spmd.sunk | while | flops 147472 | bytes 1819669 | solution.py:98
  402.9 7.2 fusion.99
  410.5 4.0 select_reduce_fusion.3
  417.7 5.5 multiply_subtract_fusion.3
  426.2 133.0 %while.65 = (s32[]{:T(128)}, f32[8,384]{1,0:T(8,128)S(1)}, f32[32,16,8,384]{3,2,1,0:T(8,128)}, pred[32,16,8,384]{3,2,1,0:T(8,128)(4,1)S(1)}, f32[32,16,8,384]{3,...) while((s32[]{:T(128)}, f32[8,384]{1,0:T(8,128)S(1)}, ...), condition=%wide.region_4.4_spmd, body=%wide.region_3.3_spmd.sunk | while | flops 147472 | bytes 1819669 | solution.py:98
  559.2 7.2 fusion.99
  566.7 4.0 select_reduce_fusion.3
  574.0 5.5 multiply_subtract_fusion.3
  582.4 133.0 %while.65 = (s32[]{:T(128)}, f32[8,384]{1,0:T(8,128)S(1)}, f32[32,16,8,384]{3,2,1,0:T(8,128)}, pred[32,16,8,384]{3,2,1,0:T(8,128)(4,1)S(1)}, f32[32,16,8,384]{3,...) while((s32[]{:T(128)}, f32[8,384]{1,0:T(8,128)S(1)}, ...), condition=%wide.region_4.4_spmd, body=%wide.region_3.3_spmd.sunk | while | flops 147472 | bytes 1819669 | solution.py:98
  715.4 7.2 fusion.99
  727.9 7.6 all-to-all-start.2
  736.8 11.4 %all-reduce.18 = (f32[]{:T(128)}, f32[]{:T(128)}) all-reduce(f32[]{:T(128)} %reduce_sum.81, f32[]{:T(128)S(6)} %convert_element_type.49), channel_id=1, replica_groups=mesh['dp_0'=4,'dp_1'=2,'seq_0'=4,'seq_1'=8] {'dp_0'}, use_global_device_ids=true, to_apply=%region_11.12 | all-reduce | flops 2 | bytes 16 | tf_op jit(solution)/shard_map/psum | solution.py:36
  751.3 11.1 %all-reduce.17 = (f32[]{:T(128)}, f32[]{:T(128)}) all-reduce(f32[]{:T(128)} %get-tuple-element.612, f32[]{:T(128)} %get-tuple-element.613), channel_id=1, replica_groups=mesh['dp_0'=4,'dp_1'=2,'seq_0'=4,'seq_1'=8] {'seq_0'}, use_global_device_ids=true, to_apply=%region_13.14 | all-reduce | flops 2 | bytes 16 | tf_op jit(solution)/shard_map/psum | solution.py:36
  762.4 16.3 %all-reduce.16 = (f32[]{:T(128)}, f32[]{:T(128)}) all-reduce(f32[]{:T(128)} %get-tuple-element.608, f32[]{:T(128)} %get-tuple-element.609), channel_id=1, replica_groups=mesh['dp_0'=4,'dp_1'=2,'seq_0'=4,'seq_1'=8] {'seq_1'}, use_global_device_ids=true, to_apply=%region_14.15 | all-reduce | flops 2 | bytes 16 | tf_op jit(solution)/shard_map/psum | solution.py:36
  (1821 shorter events, 442.0 us)
Async XLA Ops:
  0.6 3.3 copy-start.2
  11.8 82.2 %all-to-all-start.1 = ((bf16[256,12,384]{2,1,0:T(8,128)(2,1)}), bf16[256,12,384]{2,1,0:T(8,128)(2,1)S(1)}, u32[]{:S(2)}, u32[]{:S(2)}) async-start(bf16[256,12,384]{2,1,0:T(8,128)(2,1)} %pad_maximum_fusion), calls=%async_computation.1 | async-start | bytes 6291456 | tf_op jit(solution)/shard_map/all_to_all | solution.py:28
  32.0 71.6 %copy-start.3 = (s32[256]{0:T(256)S(1)}, s32[256]{0:T(256)}, u32[]{:S(2)}) copy-start(s32[256]{0:T(256)} %param.12) | copy-start | bytes 3076
  32.0 71.6 %copy-start.4 = (s32[256]{0:T(256)S(1)}, s32[256]{0:T(256)}, u32[]{:S(2)}) copy-start(s32[256]{0:T(256)} %param.13) | copy-start | bytes 3076
  94.0 150.0 %all-to-all-start = ((bf16[256,48,192]{2,1,0:T(8,128)(2,1)}), bf16[256,48,192]{2,1,0:T(8,128)(2,1)}, u32[]{:S(2)}, u32[]{:S(2)}) async-start(bf16[256,48,192]{2,1,0:T(8,128)(2,1)} %copy.42), calls=%async_computation | async-start | bytes 12582912 | tf_op jit(solution)/shard_map/all_to_all | solution.py:132
  258.2 3.2 copy-start
  410.5 4.0 copy-start.1
  414.5 3.2 copy-start
  566.7 4.0 copy-start.1
  570.7 3.2 copy-start
  723.0 4.0 copy-start.1
  727.9 51.9 %all-to-all-start.2 = ((f32[32,1,384]{2,1,0:T(1,128)}), f32[32,1,384]{2,1,0:T(1,128)S(1)}, u32[]{:S(2)}, u32[]{:S(2)}) async-start(f32[32,1,384]{2,1,0:T(1,128)} %reshape.402), calls=%async_computation.2 | async-start | bytes 98304 | tf_op jit(solution)/shard_map/all_to_all | solution.py:139
where the time goes:
time: 790 us; the launch traced here: 783 us
  local copies, waits for them, and re-layouts  313 us (40%)
  waiting for transfers between devices  195 us (25%)
  other arithmetic  174 us (22%)
  blocking collectives  41.8 us (5%)
  starting transfers between devices  28.5 us (4%)
  matrix products  26.2 us (3%)
    slice x96, local copies, waits for them, and re-layouts, one_block(): lax.scan(one_frame, previous, (jnp.moveaxis(loglik, 1, 0), jnp.moveaxis(a...  209 us
    all_to_all x1, waiting for transfers between devices, shards(): lax.all_to_all(latents, SEQ, split_axis=0, concat_axis=1, tiled=True)  133 us
    while x1440, other arithmetic  114 us
    dynamic_update_slice x96, local copies, waits for them, and re-layouts, one_block(): lax.scan(one_frame, previous, (jnp.moveaxis(loglik, 1, 0), jnp.moveaxis(a...  66.9 us
    all_to_all x1, waiting for transfers between devices, in_one_piece(): lax.all_to_all(both, axis, split_axis=split_dim, concat_axis=concat_dim,...  61.9 us
    psum x4, blocking collectives, over_axes(): return functools.reduce(lax.psum, axes, shard)  41.8 us
    unnamed x15, local copies, waits for them, and re-layouts  28.8 us
    sub x3, other arithmetic, one_block(): weight = jnp.exp(block_scores - summit)  21.5 us
  transfers between devices with their start and end apart: 3, of which 2 were waited for; matrix products, arithmetic and copies ran while one was open for 2% of the time, Pallas kernels for 0%

commit v1 on v0

v1 whole, which is shorter than its diff:
```python
import functools
import math

import jax
import jax.numpy as jnp
from jax import lax
from jax.experimental import pallas as pl
from jax.experimental.pallas import tpu as pltpu
from jax.sharding import Mesh
from jax.sharding import PartitionSpec as P

SEQ = ("seq_0", "seq_1")
DP = ("dp_0", "dp_1")

C = 192
TXT = 384
FR = 1536
OWN = 32
GRP = 256
TB = TXT // OWN
FB = FR // OWN
NU = 4
NCH = GRP // OWN // NU
ROWS = (NU + NU // 2) * FB
PROWS = (GRP // OWN) * 3 // 2 * TB
PAD = 296
NK = 2 * (NU + NU // 2) * 128
NN = TB * 128
MB = 384

HALF_LOG_TWO_PI = 0.9189385332046727
NEG = -2.0e11
F32 = jnp.float32
BF16 = jnp.bfloat16
NT = (((1,), (1,)), ((), ()))
NN_DIMS = (((1,), (0,)), ((), ()))


def params():
    return pltpu.CompilerParams(vmem_limit_bytes=60 * 1024 * 1024)


def call(body, out_shape, n_in, scratch=(), smem=()):
    vmem = pl.BlockSpec(memory_space=pltpu.VMEM)
    return pl.pallas_call(
        body,
        out_shape=out_shape,
        in_specs=[pl.BlockSpec(memory_space=pltpu.SMEM) if i in smem else vmem for i in range(n_in)],
        out_specs=jax.tree.map(lambda _: vmem, out_shape),
        scratch_shapes=list(scratch),
        compiler_params=params(),
    )


def one_hot(rank_row, first, count, dtype):
    ids = lax.broadcasted_iota(jnp.int32, (count, GRP), 0) + first
    return jnp.where(ids == rank_row, 1.0, 0.0).astype(dtype)


def pack_block(x, picks, stage, at, pair_at, step, count):
    got = lax.dot_general(picks, x, NT, preferred_element_type=F32)
    for k in range(count):
        stage[pl.ds(at + k * step, OWN, stride=PAD), :] = got[k * OWN : (k + 1) * OWN, 0:128]
    for p in range(count // 2):
        low = got[2 * p * OWN : (2 * p + 1) * OWN, 128:C]
        high = got[(2 * p + 1) * OWN : (2 * p + 2) * OWN, 128:C]
        stage[pl.ds(pair_at + p * step, OWN, stride=PAD), :] = jnp.concatenate([low, high], axis=1)


def unstage(stage, out_ref, rows):
    for d in range(OWN):
        out_ref[d] = stage[d * PAD : d * PAD + rows, :].astype(BF16)


def pack_priors(rank_ref, means_ref, logs_ref, out_ref, stage):
    picks = one_hot(rank_ref[...], 0, GRP, BF16)
    count = GRP // OWN

    def token(i, _):
        for which, ref in enumerate((means_ref, logs_ref)):
            at = which * PROWS + i
            pack_block(ref[i], picks, stage, at, at + count * TB, TB, count)
        return 0

    lax.fori_loop(0, TB, token, 0)
    unstage(stage, out_ref, 2 * PROWS)


def pack_latents(chunk, rank_ref, lat_ref, out_ref, stage):
    picks = one_hot(rank_ref[...], chunk * NU * OWN, NU * OWN, BF16)

    def frame(j, _):
        pack_block(lat_ref[j], picks, stage, j, j + NU * FB, FB, NU)
        return 0

    lax.fori_loop(0, FB, frame, 0)
    unstage(stage, out_ref, ROWS)


def build_sides(chunk, y_ref, text_ref, rhs_ref, bias_ref, wt, pr, zz, zs):
    wide = 152
    for s in range(OWN):
        m = y_ref[s, 0:PROWS, :].astype(F32)
        ls = y_ref[s, PROWS : 2 * PROWS, :].astype(F32)
        prec = jnp.exp(-2.0 * ls)
        wt[s * wide : s * wide + PROWS, :] = m * prec
        pr[s * wide : s * wide + PROWS, :] = prec
        zz[s * wide : s * wide + PROWS, :] = 0.5 * (m * m * prec) + ls
    rhs_ref[...] = jnp.zeros((NN, NK), BF16)
    lane = lax.broadcasted_iota(jnp.int32, (OWN, 128), 1)
    half = NK // 2 // 128
    count = GRP // OWN
    for i in range(TB):
        for k in range(NU):
            rows = pl.ds((chunk * NU + k) * TB + i, OWN, stride=wide)
            pairs = pl.ds((count + chunk * NU // 2 + k // 2) * TB + i, OWN, stride=wide)
            keep = (lane < 64) if k % 2 == 0 else (lane >= 64)
            at = slice(i * 128 + k * OWN, i * 128 + (k + 1) * OWN)
            for off, ref, scale in ((0, wt, 1.0), (half, pr, -0.5)):
                a = ref[rows, :].astype(BF16)
                b = jnp.where(keep, ref[pairs, :], 0.0).astype(BF16)
                q = (off + k) * 128
                rhs_ref[at, q : q + 128] = a * jnp.asarray(scale, BF16)
                q = (off + NU + k // 2) * 128
                rhs_ref[at, q : q + 128] = b * jnp.asarray(scale, BF16)
            zs[at, :] = zz[rows, :] + jnp.where(keep, zz[pairs, :], 0.0)
    ones = jnp.ones((8, 128), F32)
    lane8 = lax.broadcasted_iota(jnp.int32, (8, 128), 1)
    text = text_ref[...]
    for i in range(TB):
        total = lax.dot_general(
            ones, zs[i * 128 : (i + 1) * 128, :], NT, precision=lax.Precision.HIGHEST, preferred_element_type=F32
        )
        token = (lane8 % OWN) * TB + i
        bias_ref[:, i * 128 : (i + 1) * 128] = jnp.where(token < text, -total - C * HALF_LOG_TWO_PI, NEG)


def search(count_ref, y_ref, rhs_ref, bias_ref, text_ref, frame_ref, out_ref, lhs, lik, buf0, buf1):
    out_ref[...] = jnp.zeros(out_ref.shape, F32)
    blocks = NK // 2 // 128
    per = MB // FB

    def matmul_block(b, _):
        for q in range(per):
            s = b * per + q
            for k in range(blocks):
                x = y_ref[s, k * FB : (k + 1) * FB, :]
                lhs[q * FB : (q + 1) * FB, k * 128 : (k + 1) * 128] = x
                wide = x.astype(F32)
                lhs[q * FB : (q + 1) * FB, (blocks + k) * 128 : (blocks + k + 1) * 128] = (wide * wide).astype(BF16)
        for t in range(NN // 256):
            got = lax.dot_general(
                lhs[...], rhs_ref[t * 256 : (t + 1) * 256, :], NT, preferred_element_type=F32
            )
            bias = bias_ref[0:1, t * 256 : (t + 1) * 256]
            lik[pl.ds(b * (MB // 8), MB // 8), :, t * 256 : (t + 1) * 256] = (got + bias).reshape(MB // 8, 8, 256)
        return 0

    lax.fori_loop(0, count_ref[0], matmul_block, 0)

    lane = lax.broadcasted_iota(jnp.int32, (8, 128), 1)
    sub = lax.broadcasted_iota(jnp.int32, (8, 128), 0)
    block = lane % OWN
    seg = lane // OWN
    lane1 = lax.broadcasted_iota(jnp.int32, (1, 128), 1)
    first1 = (lane1 % OWN) == 0
    block_start = (block * TB).astype(F32)
    text = text_ref[...]
    frames = frame_ref[...]
    base = block * TB + frames - text
    inverse = 1.0 / (text - 1).astype(F32)
    scale = math.log2(math.e) / C

    def run_frames(at, state, buf, opening):
        for j in range(FB):
            entering = jnp.where(first1, opening if j == 0 else NEG, pltpu.roll(state[TB - 1], 1, 1))
            new = []
            for i in range(TB):
                like = lik[at + j // 8, j % 8 : j % 8 + 1, i * 128 : (i + 1) * 128]
                before = entering if i == 0 else state[i - 1]
                now = like + jnp.maximum(state[i], before)
                buf[j : j + 1, i * 128 : (i + 1) * 128] = now
                new.append(now)
            state = new
        return state

    def by_segment(x, reduce, fill):
        out = None
        for k in range(NU):
            one = reduce(jnp.where(seg == k, x, fill), axis=1, keepdims=True)
            out = jnp.broadcast_to(one, (8, 128)) if out is None else jnp.where(seg == k, one, out)
        return out

    def soften(index, buf, finish):
        rows = []
        for g in range(FB // 8):
            frame = index * FB + g * 8 + sub
            late = frame - base
            xs = [
                jnp.where(late <= i, buf[g * 8 : (g + 1) * 8, i * 128 : (i + 1) * 128], 8 * NEG)
                for i in range(TB)
            ]
            top = by_segment(functools.reduce(jnp.maximum, xs), jnp.max, -3.0e38)
            ws = [jnp.exp2((x - top) * scale) for x in xs]
            suffix = ws[TB - 1]
            moment = suffix
            for i in range(TB - 2, 0, -1):
                suffix = suffix + ws[i]
                moment = moment + suffix
            weight = suffix + ws[0]
            moment = moment + block_start * weight
            weight = by_segment(weight, jnp.sum, 0.0)
            moment = by_segment(moment, jnp.sum, 0.0)
            rows.append(jnp.where(frame < frames, moment / weight * inverse, 0.0))
            finish = finish + jnp.where(frame == frames - 1, top, 0.0)
        turned = jnp.concatenate(rows + [jnp.zeros((128 - FB, 128), F32)], axis=0).T
        where = jnp.maximum(index, 0)
        for k in range(NU):
            out_ref[where, k : k + 1, :] = turned[k * OWN : k * OWN + 1, :]
        return finish

    def pair(b, carried):
        state, finish = list(carried[:TB]), carried[TB]
        state = run_frames(b * (2 * FB // 8), state, buf0, jnp.where(b == 0, 0.0, NEG))
        finish = soften(2 * b - 1, buf1, finish)
        state = run_frames(b * (2 * FB // 8) + FB // 8, state, buf1, NEG)
        finish = soften(2 * b, buf0, finish)
        return (*state, finish)

    start = [jnp.full((1, 128), NEG, F32) for _ in range(TB)]
    carried = lax.fori_loop(0, count_ref[1], pair, (*start, jnp.zeros((8, 128), F32)))
    finish = soften(2 * count_ref[1] - 1, buf1, carried[TB])
    finish = jnp.sum(finish, axis=0, keepdims=True) * (1.0 / C)
    for d in range(OWN):
        out_ref[d, NU : NU + 1, :] = finish


def unpack(rank_ref, a_ref, b_ref, pos_ref, finish_ref, turned):
    lane1 = lax.broadcasted_iota(jnp.int32, (1, 128), 1)
    finish = jnp.zeros((1, 128), F32)
    for c, ref in enumerate((a_ref, b_ref)):
        rows = [ref[pl.ds(k, OWN, stride=8), :] for k in range(NU)]
        turned[:, c * 128 : (c + 1) * 128] = jnp.concatenate(rows, axis=0).T
        finish = finish + jnp.sum(ref[pl.ds(NU, OWN, stride=8), :], axis=0, keepdims=True)
    picks = one_hot(rank_ref[...], 0, GRP, F32)
    pos_ref[...] = lax.dot_general(
        turned[0:FB, :], picks, NN_DIMS, precision=lax.Precision.HIGHEST, preferred_element_type=F32
    )
    finish = jnp.sum(jnp.where(lane1 % OWN == 0, finish, 0.0), axis=1, keepdims=True)
    finish_ref[...] = jnp.broadcast_to(finish, (8, 128))


def exchange(x):
    return lax.all_to_all(x, SEQ, split_axis=0, concat_axis=0, tiled=True)


def make_rhs(chunk, prior, text_lanes):
    wide = pltpu.VMEM((OWN * 152, 128), F32)
    return call(
        functools.partial(build_sides, chunk),
        (jax.ShapeDtypeStruct((NN, NK), BF16), jax.ShapeDtypeStruct((8, NN), F32)),
        2,
        (wide, wide, wide, pltpu.VMEM((NN, 128), F32)),
    )(prior, text_lanes)


def run_search(counts, got, rhs, bias, text_lanes, frame_lanes):
    return call(
        search,
        jax.ShapeDtypeStruct((OWN, 8, 128), F32),
        6,
        (
            pltpu.VMEM((MB, NK), BF16),
            pltpu.VMEM((FR // 8, 8, NN), F32),
            pltpu.VMEM((FB, NN), F32),
            pltpu.VMEM((FB, NN), F32),
        ),
        smem=(0,),
    )(counts, got, rhs, bias, text_lanes, frame_lanes)


def pack_call(body, rank, arrays, rows):
    return call(
        body, jax.ShapeDtypeStruct((OWN, rows, 128), BF16), 1 + len(arrays), (pltpu.VMEM((OWN * PAD, 128), F32),)
    )(rank, *arrays)


def ranks(frame_lens):
    ids = jnp.arange(GRP, dtype=jnp.int32)
    a, b = frame_lens[:, None], frame_lens[None, :]
    ahead = (a > b) | ((a == b) & (ids[:, None] < ids[None, :]))
    return jnp.sum(ahead.astype(jnp.int32), axis=0)[None, :]


def owned(lens, rank, own):
    slots = jnp.arange(GRP // OWN, dtype=jnp.int32) * OWN + own
    return jnp.sum(jnp.where(rank == slots[:, None], lens[None, :], 0), axis=1)


def lanes_of(lens, chunk):
    part = lens[chunk * NU : (chunk + 1) * NU]
    return jnp.broadcast_to(jnp.repeat(part, OWN)[None, :], (8, 128))


def shards(means, log_scales, latents, text_lens, frame_lens):
    own = lax.axis_index(SEQ).astype(jnp.int32)
    rank = ranks(frame_lens)
    text_own, frame_own = owned(text_lens, rank, own), owned(frame_lens, rank, own)
    lat = jnp.transpose(latents, (1, 2, 0))
    turn = lambda x: jnp.transpose(x, (1, 2, 0))
    prior = exchange(pack_call(pack_priors, rank, (turn(means), turn(log_scales)), 2 * PROWS))
    got = [
        exchange(pack_call(functools.partial(pack_latents, c), rank, (lat,), ROWS)) for c in range(NCH)
    ]
    back = []
    for c in range(NCH):
        text_lanes, frame_lanes = lanes_of(text_own, c), lanes_of(frame_own, c)
        longest = jnp.max(frame_own[c * NU : (c + 1) * NU])
        counts = jnp.stack([(longest + MB - 1) // MB, (longest + 2 * FB - 1) // (2 * FB)])
        rhs, bias = make_rhs(c, prior, text_lanes)
        back.append(exchange(run_search(counts, got[c], rhs, bias, text_lanes, frame_lanes)))
    pos, finish = call(
        unpack,
        (jax.ShapeDtypeStruct((FB, GRP), F32), jax.ShapeDtypeStruct((8, 128), F32)),
        3,
        (pltpu.VMEM((128, 2 * 128), F32),),
    )(rank, *(b.reshape(OWN * 8, 128) for b in back))
    frame_total = lax.psum(jnp.sum(frame_lens).astype(F32), DP)
    path_total = lax.psum(finish[0, 0], DP)
    return (jnp.transpose(pos), -path_total / frame_total)


def solution(mesh):
    torus = Mesh(mesh.devices.reshape(4, 2, 4, 8), ("dp_0", "dp_1", "seq_0", "seq_1"))
    in_specs = (P(DP, SEQ, None), P(DP, SEQ, None), P(DP, SEQ, None), P(DP), P(DP))
    out_specs = (P(DP, SEQ), P())
    return jax.shard_map(
        shards, mesh=torus, in_specs=in_specs, out_specs=out_specs, check_vma=False
    )
```

time: 790 us -> 290 us (0.37)
  local copies, waits for them, and re-layouts: 313 us -> 7.8 us
  other arithmetic: 174 us -> 4.21 us
  Pallas kernels: 0 us -> 108 us
  waiting for transfers between devices: 195 us -> 106 us
  blocking collectives: 41.8 us -> 13.2 us
  matrix products: 26.2 us -> 0 us
  starting transfers between devices: 28.5 us -> 41.7 us
    slice x96 -> x1, local copies, waits for them, and re-layouts: 209 us -> 1.19 us  [shards(): path_total = lax.psum(finish[0, 0], DP)]
    while x1440 -> x0, other arithmetic: 114 us -> none
    pallas_call x0 -> x8, Pallas kernels: none -> 108 us  [the longest x2 55.2 us: run_search(): call(search, jax.ShapeDtypeStruct((OWN, 8, 128), F32), 6, (pltpu.VMEM((MB...]
    all_to_all x3 -> x5, waiting for transfers between devices: 195 us -> 106 us  [exchange(): return lax.all_to_all(x, SEQ, split_axis=0, concat_axis=0, tiled=True)]
    dynamic_update_slice x96 -> x0, local copies, waits for them, and re-layouts: 66.9 us -> none  [one_block(): lax.scan(one_frame, previous, (jnp.moveaxis(loglik, 1, 0), jnp.moveaxis(a...]
    psum x4 -> x1, blocking collectives: 41.8 us -> 13.2 us  [shards(): path_total = lax.psum(finish[0, 0], DP)]
    dot_general x6 -> x0, matrix products: 26.2 us -> none  [the longest x3 16.6 us: block_loglik(): lax.dot_general(squared_latent, prec_low, PAIR_DIMS, preferred_element_ty...]
    unnamed x15 -> x14, local copies, waits for them, and re-layouts: 28.8 us -> 3.63 us
  transfers between devices with their start and end apart: 3 -> 5, of which waited for: 2 -> 4; matrix products, arithmetic and copies ran while one was open for 2% -> 2% of each run, Pallas kernels for 0% -> 31%
where the time goes in v1:
time: 290 us; the launch traced here: 288 us
  Pallas kernels  108 us (37%)
  waiting for transfers between devices  106 us (37%)
  starting transfers between devices  41.7 us (14%)
  blocking collectives  13.2 us (5%)
  local copies, waits for them, and re-layouts  7.8 us (3%)
  between operations  6.49 us (2%)
  other arithmetic  4.21 us (1%)
    all_to_all x5, waiting for transfers between devices, exchange(): return lax.all_to_all(x, SEQ, split_axis=0, concat_axis=0, tiled=True)  106 us
    pallas_call x2, Pallas kernels, run_search(): call(search, jax.ShapeDtypeStruct((OWN, 8, 128), F32), 6, (pltpu.VMEM((MB...  55.2 us
    all_to_all x5, starting transfers between devices, exchange(): return lax.all_to_all(x, SEQ, split_axis=0, concat_axis=0, tiled=True)  41.7 us
    pallas_call x3, Pallas kernels, pack_call(): call(body, jax.ShapeDtypeStruct((OWN, rows, 128), BF16), 1 + len(arrays),...  39.8 us
    psum x1, blocking collectives, shards(): path_total = lax.psum(finish[0, 0], DP)  13.2 us
    pallas_call x2, Pallas kernels, make_rhs(): call(functools.partial(build_sides, chunk), (jax.ShapeDtypeStruct((NN, NK...  10.8 us
  transfers between devices with their start and end apart: 5, of which 4 were waited for; matrix products, arithmetic and copies ran while one was open for 2% of the time, Pallas kernels for 31%

profile of v1, /device:TPU:32, one launch (start us, length us, event | category | flops | bytes accessed | tf_op | source)
XLA Modules:
  0.0 287.6 jit_solution(11522252795071923518)
XLA Ops:
  0.6 1.4 convert_reduce_fusion
  2.0 16.3 %shard_map.68 = bf16[32,288,128]{2,1,0:T(8,128)(2,1)} custom-call(s32[1,256]{1,0:T(1,128)} %bitcast.18, bf16[48,192,256]{2,1,0:T(8,128)(2,1)} %bitcast.12), custom_call_target="tpu_custom_call" | custom-call | tf_op jit(solution)/shard_map/pallas_call | solution.py:283
  18.4 11.2 %all-to-all-start = ((bf16[32,288,128]{2,1,0:T(8,128)(2,1)}), bf16[32,288,128]{2,1,0:T(8,128)(2,1)S(1)}, u32[]{:S(2)}, u32[]{:S(2)}) async-start(bf16[32,288,128]{2,1,0:T(8,128)(2,1)} %shard_map.68), calls=%async_computation | async-start | bytes 4718592 | tf_op jit(solution)/shard_map/all_to_all | solution.py:254
  29.6 7.1 %shard_map.69 = bf16[32,288,128]{2,1,0:T(8,128)(2,1)} custom-call(s32[1,256]{1,0:T(1,128)} %bitcast.19, bf16[12,192,256]{2,1,0:T(8,128)(2,1)} %bitcast.14, bf16[12,192,256]{2,1,0:T(8,128)(2,1)} %bitcast.15), custom_call_target="tpu_custom_call" | custom-call | tf_op jit(solution)/shard_map/pallas_call | solution.py:283
  36.7 47.3 %all-to-all-done.y_ref = bf16[32,288,128]{2,1,0:T(8,128)(2,1)S(1)} async-done(((bf16[32,288,128]{2,1,0:T(8,128)(2,1)}), bf16[32,288,128]{2,1,0:T(8,128)(2,1)S(1)}, u32[]{:S(2)}, u32[]{:S(2)}) %all-to-all-start) | async-done | bytes 2359328 | tf_op jit(solution)/shard_map/all_to_all | solution.py:254
  84.0 1.5 copy-done.1
  85.5 7.3 %all-to-all-start.1 = ((bf16[32,288,128]{2,1,0:T(8,128)(2,1)}), bf16[32,288,128]{2,1,0:T(8,128)(2,1)S(1)}, u32[]{:S(2)}, u32[]{:S(2)}) async-start(bf16[32,288,128]{2,1,0:T(8,128)(2,1)} %shard_map.69), calls=%async_computation.1 | async-start | bytes 4718592 | tf_op jit(solution)/shard_map/all_to_all | solution.py:254
  92.9 16.3 %shard_map.72 = bf16[32,288,128]{2,1,0:T(8,128)(2,1)} custom-call(s32[1,256]{1,0:T(1,128)} %bitcast.20, bf16[48,192,256]{2,1,0:T(8,128)(2,1)} %bitcast.13), custom_call_target="tpu_custom_call" | custom-call | tf_op jit(solution)/shard_map/pallas_call | solution.py:283
  109.2 38.0 %all-to-all-done.1.y_ref = bf16[32,288,128]{2,1,0:T(8,128)(2,1)S(1)} async-done(((bf16[32,288,128]{2,1,0:T(8,128)(2,1)}), bf16[32,288,128]{2,1,0:T(8,128)(2,1)S(1)}, u32[]{:S(2)}, u32[]{:S(2)}) %all-to-all-start.1) | async-done | bytes 2359328 | tf_op jit(solution)/shard_map/all_to_all | solution.py:254
  147.2 1.5 copy-done
  148.6 7.4 %all-to-all-start.3 = ((bf16[32,288,128]{2,1,0:T(8,128)(2,1)}), bf16[32,288,128]{2,1,0:T(8,128)(2,1)}, u32[]{:S(2)}, u32[]{:S(2)}) async-start(bf16[32,288,128]{2,1,0:T(8,128)(2,1)} %shard_map.72), calls=%async_computation.3 | async-start | bytes 4718592 | tf_op jit(solution)/shard_map/all_to_all | solution.py:254
  156.2 0.7 slice_reduce_fusion
  159.8 5.6 %shard_map.70 = (bf16[1536,1536]{1,0:T(8,128)(2,1)}, f32[8,1536]{1,0:T(8,128)}) custom-call(bf16[32,288,128]{2,1,0:T(8,128)(2,1)} %copy-done, s32[8,128]{1,0:T(8,128)} %broadcast_in_dim.75.text_ref), custom_call_target="tpu_custom_call" | custom-call | tf_op jit(solution)/shard_map/pallas_call | solution.py:259
  165.9 31.5 %shard_map.71 = f32[32,8,128]{2,1,0:T(8,128)} custom-call(s32[2]{0:T(128)} %pad_add_fusion.count_ref, bf16[32,288,128]{2,1,0:T(8,128)(2,1)} %copy-done.1, bf16[1536,1536]{1,0:T(8,128)(2,1)} %get-tuple-element.8.rhs_ref, f32[8,1536]{1,0:T(8,128)} %get-tuple-element.9.bias_ref, s32[8,128]{1,0:T(8,128)} %broadcast_in_dim.75.text_ref, ...), custom_call_target="tpu_custom_call" | custom-call | tf_op jit(solution)/shard_map/pallas_call | solution.py:268
  197.5 12.8 %all-to-all-done.3.y_ref = bf16[32,288,128]{2,1,0:T(8,128)(2,1)} async-done(((bf16[32,288,128]{2,1,0:T(8,128)(2,1)}), bf16[32,288,128]{2,1,0:T(8,128)(2,1)}, u32[]{:S(2)}, u32[]{:S(2)}) %all-to-all-start.3) | async-done | bytes 2359328 | tf_op jit(solution)/shard_map/all_to_all | solution.py:254
  210.2 7.3 %all-to-all-start.2 = ((f32[32,8,128]{2,1,0:T(8,128)}), f32[32,8,128]{2,1,0:T(8,128)S(1)}, u32[]{:S(2)}, u32[]{:S(2)}) async-start(f32[32,8,128]{2,1,0:T(8,128)} %shard_map.71), calls=%async_computation.2 | async-start | bytes 262144 | tf_op jit(solution)/shard_map/all_to_all | solution.py:254
  219.2 0.7 pad_add_fusion.1.count_ref
  220.4 5.2 %shard_map.73 = (bf16[1536,1536]{1,0:T(8,128)(2,1)}, f32[8,1536]{1,0:T(8,128)}) custom-call(bf16[32,288,128]{2,1,0:T(8,128)(2,1)} %copy-done, s32[8,128]{1,0:T(8,128)} %broadcast_in_dim.81.text_ref), custom_call_target="tpu_custom_call" | custom-call | tf_op jit(solution)/shard_map/pallas_call | solution.py:259
  226.2 23.7 %shard_map.74 = f32[32,8,128]{2,1,0:T(8,128)} custom-call(s32[2]{0:T(128)} %pad_add_fusion.1.count_ref, bf16[32,288,128]{2,1,0:T(8,128)(2,1)} %all-to-all-done.3.y_ref, bf16[1536,1536]{1,0:T(8,128)(2,1)} %get-tuple-element.10.rhs_ref, f32[8,1536]{1,0:T(8,128)} %get-tuple-element.11.bias_ref, s32[8,128]{1,0:T(8,128)} %broadcast_in_dim.81.text_ref, ...), custom_call_target="tpu_custom_call" | custom-call | tf_op jit(solution)/shard_map/pallas_call | solution.py:268
  249.9 8.6 %all-to-all-start.4 = ((f32[32,8,128]{2,1,0:T(8,128)}), f32[32,8,128]{2,1,0:T(8,128)S(1)}, u32[]{:S(2)}, u32[]{:S(2)}) async-start(f32[32,8,128]{2,1,0:T(8,128)} %shard_map.74), calls=%async_computation.4 | async-start | bytes 262144 | tf_op jit(solution)/shard_map/all_to_all | solution.py:254
  259.8 8.4 %all-to-all-done.4 = f32[32,8,128]{2,1,0:T(8,128)S(1)} async-done(((f32[32,8,128]{2,1,0:T(8,128)}), f32[32,8,128]{2,1,0:T(8,128)S(1)}, u32[]{:S(2)}, u32[]{:S(2)}) %all-to-all-start.4) | async-done | bytes 131104 | tf_op jit(solution)/shard_map/all_to_all | solution.py:254
  268.8 1.9 shard_map.75
  270.7 1.2 slice.21
  271.9 13.2 %all-reduce = (f32[]{:T(128)}, f32[]{:T(128)}) all-reduce(f32[]{:T(128)} %bitcast.11, f32[]{:T(128)S(6)} %convert_element_type.7), channel_id=1, replica_groups=mesh['dp_0'=4,'dp_1'=2,'seq_0'=4,'seq_1'=8] {'dp_0','dp_1'}, use_global_device_ids=true, to_apply=%region_5.6 | all-reduce | flops 2 | bytes 16 | tf_op jit(solution)/shard_map/psum | solution.py:329
  (29 shorter events, 5.1 us)
Async XLA Ops:
  18.4 65.7 %all-to-all-start = ((bf16[32,288,128]{2,1,0:T(8,128)(2,1)}), bf16[32,288,128]{2,1,0:T(8,128)(2,1)S(1)}, u32[]{:S(2)}, u32[]{:S(2)}) async-start(bf16[32,288,128]{2,1,0:T(8,128)(2,1)} %shard_map.68), calls=%async_computation | async-start | bytes 4718592 | tf_op jit(solution)/shard_map/all_to_all | solution.py:254
  84.0 1.5 copy-start.1
  85.5 61.6 %all-to-all-start.1 = ((bf16[32,288,128]{2,1,0:T(8,128)(2,1)}), bf16[32,288,128]{2,1,0:T(8,128)(2,1)S(1)}, u32[]{:S(2)}, u32[]{:S(2)}) async-start(bf16[32,288,128]{2,1,0:T(8,128)(2,1)} %shard_map.69), calls=%async_computation.1 | async-start | bytes 4718592 | tf_op jit(solution)/shard_map/all_to_all | solution.py:254
  109.2 46.8 %copy-start.4 = (s32[256]{0:T(256)S(1)}, s32[256]{0:T(256)}, u32[]{:S(2)}) copy-start(s32[256]{0:T(256)} %convert_reduce_fusion) | copy-start | bytes 3076
  109.2 46.9 %copy-start.5 = (s32[256]{0:T(256)S(1)}, s32[256]{0:T(256)}, u32[]{:S(2)}) copy-start(s32[256]{0:T(256)} %param.9) | copy-start | bytes 3076
  109.2 46.9 %copy-start.6 = (s32[256]{0:T(256)S(1)}, s32[256]{0:T(256)}, u32[]{:S(2)}) copy-start(s32[256]{0:T(256)} %param.8) | copy-start | bytes 3076
  147.2 1.5 copy-start
  148.6 61.6 %all-to-all-start.3 = ((bf16[32,288,128]{2,1,0:T(8,128)(2,1)}), bf16[32,288,128]{2,1,0:T(8,128)(2,1)}, u32[]{:S(2)}, u32[]{:S(2)}) async-start(bf16[32,288,128]{2,1,0:T(8,128)(2,1)} %shard_map.72), calls=%async_computation.3 | async-start | bytes 4718592 | tf_op jit(solution)/shard_map/all_to_all | solution.py:254
  210.2 39.7 %all-to-all-start.2 = ((f32[32,8,128]{2,1,0:T(8,128)}), f32[32,8,128]{2,1,0:T(8,128)S(1)}, u32[]{:S(2)}, u32[]{:S(2)}) async-start(f32[32,8,128]{2,1,0:T(8,128)} %shard_map.71), calls=%async_computation.2 | async-start | bytes 262144 | tf_op jit(solution)/shard_map/all_to_all | solution.py:254
  249.9 18.3 %copy-start.2 = (f32[32,8,128]{2,1,0:T(8,128)}, f32[32,8,128]{2,1,0:T(8,128)S(1)}, u32[]{:S(2)}) copy-start(f32[32,8,128]{2,1,0:T(8,128)S(1)} %all-to-all-done.2) | copy-start | bytes 393220
  249.9 18.2 %all-to-all-start.4 = ((f32[32,8,128]{2,1,0:T(8,128)}), f32[32,8,128]{2,1,0:T(8,128)S(1)}, u32[]{:S(2)}, u32[]{:S(2)}) async-start(f32[32,8,128]{2,1,0:T(8,128)} %shard_map.74), calls=%async_computation.4 | async-start | bytes 262144 | tf_op jit(solution)/shard_map/all_to_all | solution.py:254
  268.1 0.6 copy-start.3

commit v2 on v1

v2 whole, which is shorter than its diff:
```python
import functools
import math

import jax
import jax.numpy as jnp
from jax import lax
from jax.experimental import pallas as pl
from jax.experimental.pallas import tpu as pltpu
from jax.sharding import Mesh
from jax.sharding import PartitionSpec as P

SEQ = ("seq_0", "seq_1")
DP = ("dp_0", "dp_1")

C = 192
TXT = 384
FR = 1536
OWN = 32
GRP = 256
TB = TXT // OWN
FB = FR // OWN
NU = 4
NCH = GRP // OWN // NU
ROWS = (NU + NU // 2) * FB
PROWS = (GRP // OWN) * 3 // 2 * TB
PAD = 296
KP = 2 * 3 * 128
UNROLL = 4
NN = TB * 128
MB = 384

HALF_LOG_TWO_PI = 0.9189385332046727
NEG = -2.0e11
F32 = jnp.float32
BF16 = jnp.bfloat16
NT = (((1,), (1,)), ((), ()))
NN_DIMS = (((1,), (0,)), ((), ()))


def params():
    return pltpu.CompilerParams(vmem_limit_bytes=60 * 1024 * 1024)


def call(body, out_shape, n_in, scratch=(), smem=()):
    vmem = pl.BlockSpec(memory_space=pltpu.VMEM)
    return pl.pallas_call(
        body,
        out_shape=out_shape,
        in_specs=[pl.BlockSpec(memory_space=pltpu.SMEM) if i in smem else vmem for i in range(n_in)],
        out_specs=jax.tree.map(lambda _: vmem, out_shape),
        scratch_shapes=list(scratch),
        compiler_params=params(),
    )


def one_hot(rank_row, first, count, dtype):
    ids = lax.broadcasted_iota(jnp.int32, (count, GRP), 0) + first
    return jnp.where(ids == rank_row, 1.0, 0.0).astype(dtype)


def pack_block(x, picks, stage, at, pair_at, step, count):
    got = lax.dot_general(picks, x, NT, preferred_element_type=F32)
    for k in range(count):
        stage[pl.ds(at + k * step, OWN, stride=PAD), :] = got[k * OWN : (k + 1) * OWN, 0:128]
    for p in range(count // 2):
        low = got[2 * p * OWN : (2 * p + 1) * OWN, 128:C]
        high = got[(2 * p + 1) * OWN : (2 * p + 2) * OWN, 128:C]
        stage[pl.ds(pair_at + p * step, OWN, stride=PAD), :] = jnp.concatenate([low, high], axis=1)


def unstage(stage, out_ref, rows):
    for d in range(OWN):
        out_ref[d] = stage[d * PAD : d * PAD + rows, :].astype(BF16)


def stage_priors(rank_ref, means_ref, logs_ref, stage):
    picks = one_hot(rank_ref[...], 0, GRP, BF16)
    count = GRP // OWN

    def tokens(i, _):
        for q in range(UNROLL // 2):
            for which, ref in enumerate((means_ref, logs_ref)):
                token = i * (UNROLL // 2) + q
                at = which * PROWS + token
                pack_block(ref[token], picks, stage, at, at + count * TB, TB, count)
        return 0

    lax.fori_loop(0, 2 * TB // UNROLL, tokens, 0)


def stage_latents(chunk, rank_ref, lat_ref, stage):
    picks = one_hot(rank_ref[...], chunk * NU * OWN, NU * OWN, BF16)

    def frames(j, _):
        for q in range(UNROLL):
            frame = j * UNROLL + q
            pack_block(lat_ref[frame], picks, stage, frame, frame + NU * FB, FB, NU)
        return 0

    lax.fori_loop(0, FB // UNROLL, frames, 0)


def unstage(stage, out_ref, first, rows):
    for d in range(OWN):
        out_ref[d, first : first + rows, :] = stage[d * PAD : d * PAD + rows, :].astype(BF16)


def pack_first(rank_ref, means_ref, logs_ref, lat_ref, out_ref, stage):
    stage_priors(rank_ref, means_ref, logs_ref, stage)
    unstage(stage, out_ref, 0, 2 * PROWS)
    stage_latents(0, rank_ref, lat_ref, stage)
    unstage(stage, out_ref, 2 * PROWS, ROWS)


def pack_second(rank_ref, lat_ref, out_ref, stage):
    stage_latents(1, rank_ref, lat_ref, stage)
    unstage(stage, out_ref, 0, ROWS)


def build_sides(y_ref, text_ref, rhs_ref, bias_ref, wt, pr, zz, zs):
    wide = 152
    for s in range(OWN):
        m = y_ref[s, 0:PROWS, :].astype(F32)
        ls = y_ref[s, PROWS : 2 * PROWS, :].astype(F32)
        prec = jnp.exp(-2.0 * ls)
        wt[s * wide : s * wide + PROWS, :] = m * prec
        pr[s * wide : s * wide + PROWS, :] = prec
        zz[s * wide : s * wide + PROWS, :] = 0.5 * (m * m * prec) + ls
    lane = lax.broadcasted_iota(jnp.int32, (OWN, 128), 1)
    none = jnp.zeros((OWN, 128), F32)
    ones = jnp.ones((8, 128), F32)
    lane8 = lax.broadcasted_iota(jnp.int32, (8, 128), 1)
    count = GRP // OWN

    def rows_of(ref, block, i):
        return ref[pl.ds(block * TB + i, OWN, stride=wide), :]

    def both(ref, pair, i):
        x = rows_of(ref, count + pair, i)
        return [jnp.where(lane < 64, x, 0.0), jnp.where(lane >= 64, x, 0.0)]

    for pair in range(count // 2):
        c, p = pair // 2, pair % 2
        for v in range(TB // 2):
            for half, (ref, factor) in enumerate(((wt, 1.0), (pr, -0.5))):
                first, second, mixed = [], [], []
                for i in (2 * v, 2 * v + 1):
                    first += [rows_of(ref, 2 * pair, i), none]
                    second += [none, rows_of(ref, 2 * pair + 1, i)]
                    mixed += both(ref, pair, i)
                for q, pieces in enumerate((first, second, mixed)):
                    turned = jnp.concatenate(pieces, axis=0).T.astype(BF16)
                    k = (half * 3 + q) * 128
                    rhs_ref[pair, k : k + 128, v * 128 : (v + 1) * 128] = turned * jnp.asarray(factor, BF16)
        for i in range(TB):
            for k, extra in enumerate(both(zz, pair, i)):
                at = c * NN + i * 128 + (2 * p + k) * OWN
                zs[at : at + OWN, :] = rows_of(zz, 2 * pair + k, i) + extra
    for c in range(NCH):
        text = text_ref[c]
        for i in range(TB):
            total = lax.dot_general(
                ones,
                zs[c * NN + i * 128 : c * NN + (i + 1) * 128, :],
                NT,
                precision=lax.Precision.HIGHEST,
                preferred_element_type=F32,
            )
            token = (lane8 % OWN) * TB + i
            bias_ref[c, :, i * 128 : (i + 1) * 128] = jnp.where(
                token < text, -total - C * HALF_LOG_TWO_PI, NEG
            )


def search(chunk, first_row, count_ref, y_ref, rhs_ref, bias_ref, text_ref, frame_ref, *rest):
    earlier, (out_ref, lhs, lik, buf0, buf1) = rest[:-5], rest[-5:]
    out_ref[...] = earlier[0][...] if earlier else jnp.zeros(out_ref.shape, F32)
    per = MB // FB
    wide_lane = lax.broadcasted_iota(jnp.int32, (MB, 128), 1)

    def matmul_block(b, _):
        for q in range(per):
            s = b * per + q
            rows = slice(q * FB, (q + 1) * FB)
            for p in range(NU // 2):
                for n, k in enumerate((2 * p, 2 * p + 1, NU + p)):
                    x = y_ref[s, first_row + k * FB : first_row + (k + 1) * FB, :]
                    at = p * KP + n * 128
                    lhs[rows, at : at + 128] = x
                    wide = x.astype(F32)
                    lhs[rows, at + 384 : at + 512] = (wide * wide).astype(BF16)
        group = pl.ds(b * (MB // 8), MB // 8)
        for t in range(KP // 256):
            got = [
                lax.dot_general(
                    lhs[:, p * KP : (p + 1) * KP],
                    rhs_ref[chunk * 2 + p, :, t * 256 : (t + 1) * 256],
                    NN_DIMS,
                    preferred_element_type=F32,
                )
                for p in range(2)
            ]
            for h in range(2):
                one, two = (g[:, h * 128 : (h + 1) * 128] for g in got)
                i = 4 * t + 2 * h
                even = jnp.where(wide_lane < 64, one, pltpu.roll(two, 64, 1))
                odd = jnp.where(wide_lane < 64, pltpu.roll(one, 64, 1), two)
                for n, x in enumerate((even, odd)):
                    cols = slice((i + n) * 128, (i + n + 1) * 128)
                    lik[group, :, cols] = (x + bias_ref[chunk, 0:1, cols]).reshape(MB // 8, 8, 128)
        return 0

    lax.fori_loop(0, count_ref[chunk], matmul_block, 0)

    lane = lax.broadcasted_iota(jnp.int32, (8, 128), 1)
    sub = lax.broadcasted_iota(jnp.int32, (8, 128), 0)
    block = lane % OWN
    seg = lane // OWN
    lane1 = lax.broadcasted_iota(jnp.int32, (1, 128), 1)
    first1 = (lane1 % OWN) == 0
    block_start = (block * TB).astype(F32)
    text = text_ref[chunk]
    frames = frame_ref[chunk]
    base = block * TB + frames - text
    inverse = 1.0 / (text - 1).astype(F32)
    scale = math.log2(math.e) / C

    def run_frames(at, state, buf, opening):
        for j in range(FB):
            entering = jnp.where(first1, opening if j == 0 else NEG, pltpu.roll(state[TB - 1], 1, 1))
            new = []
            for i in range(TB):
                like = lik[at + j // 8, j % 8 : j % 8 + 1, i * 128 : (i + 1) * 128]
                before = entering if i == 0 else state[i - 1]
                now = like + jnp.maximum(state[i], before)
                buf[j : j + 1, i * 128 : (i + 1) * 128] = now
                new.append(now)
            state = new
        return state

    def by_segment(x, reduce, fill):
        out = None
        for k in range(NU):
            one = reduce(jnp.where(seg == k, x, fill), axis=1, keepdims=True)
            out = jnp.broadcast_to(one, (8, 128)) if out is None else jnp.where(seg == k, one, out)
        return out

    def soften(index, buf, finish):
        rows = []
        for g in range(FB // 8):
            frame = index * FB + g * 8 + sub
            late = frame - base
            xs = [
                jnp.where(late <= i, buf[g * 8 : (g + 1) * 8, i * 128 : (i + 1) * 128], 8 * NEG)
                for i in range(TB)
            ]
            top = by_segment(functools.reduce(jnp.maximum, xs), jnp.max, -3.0e38)
            ws = [jnp.exp2((x - top) * scale) for x in xs]
            suffix = ws[TB - 1]
            moment = suffix
            for i in range(TB - 2, 0, -1):
                suffix = suffix + ws[i]
                moment = moment + suffix
            weight = suffix + ws[0]
            moment = moment + block_start * weight
            weight = by_segment(weight, jnp.sum, 0.0)
            moment = by_segment(moment, jnp.sum, 0.0)
            rows.append(jnp.where(frame < frames, moment / weight * inverse, 0.0))
            finish = finish + jnp.where(frame == frames - 1, top, 0.0)
        turned = jnp.concatenate(rows + [jnp.zeros((128 - FB, 128), F32)], axis=0).T
        where = jnp.maximum(index, 0)
        for k in range(NU):
            out_ref[where, chunk * NU + k : chunk * NU + k + 1, :] = turned[k * OWN : k * OWN + 1, :]
        return finish

    def pair(b, carried):
        state, finish = list(carried[:TB]), carried[TB]
        state = run_frames(b * (2 * FB // 8), state, buf0, jnp.where(b == 0, 0.0, NEG))
        finish = soften(2 * b - 1, buf1, finish)
        state = run_frames(b * (2 * FB // 8) + FB // 8, state, buf1, NEG)
        finish = soften(2 * b, buf0, finish)
        return (*state, finish)

    start = [jnp.full((1, 128), NEG, F32) for _ in range(TB)]
    carried = lax.fori_loop(0, count_ref[NCH + chunk], pair, (*start, jnp.zeros((8, 128), F32)))
    finish = soften(2 * count_ref[NCH + chunk] - 1, buf1, carried[TB])
    finish = jnp.sum(finish, axis=0, keepdims=True) * (1.0 / C)
    finish = jnp.sum(jnp.where(first1, finish, 0.0), axis=1, keepdims=True)
    for d in range(OWN):
        out_ref[d, chunk * NU : chunk * NU + 1, 64:128] = jnp.broadcast_to(finish, (1, 64))


def unpack(rank_ref, frame_ref, got_ref, pos_ref, sums_ref, turned):
    lane1 = lax.broadcasted_iota(jnp.int32, (1, 128), 1)
    rows = [got_ref[pl.ds(k, OWN, stride=8), :] for k in range(NCH * NU)]
    finish = sum(jnp.sum(rows[c * NU], axis=0, keepdims=True) for c in range(NCH))
    for c in range(2):
        turned[:, c * 128 : (c + 1) * 128] = jnp.concatenate(rows[c * 4 : c * 4 + 4], axis=0).T
    picks = one_hot(rank_ref[...], 0, GRP, F32)
    pos_ref[...] = lax.dot_general(
        turned[0:FB, :], picks, NN_DIMS, precision=lax.Precision.HIGHEST, preferred_element_type=F32
    )
    lens = jnp.sum(frame_ref[...].astype(F32), axis=1, keepdims=True)
    sums = jnp.where(lane1 >= 64, finish, lens)
    sums_ref[...] = jnp.broadcast_to(sums, (8, 128))


def exchange(x):
    return lax.all_to_all(x, SEQ, split_axis=0, concat_axis=0, tiled=True)


def make_rhs(first, text_lanes):
    wide = pltpu.VMEM((OWN * 152, 128), F32)
    return call(
        build_sides,
        (jax.ShapeDtypeStruct((NCH * 2, KP, KP), BF16), jax.ShapeDtypeStruct((NCH, 8, NN), F32)),
        2,
        (wide, wide, wide, pltpu.VMEM((NCH * NN, 128), F32)),
    )(first, text_lanes)


def run_search(chunk, first_row, *operands):
    return call(
        functools.partial(search, chunk, first_row),
        jax.ShapeDtypeStruct((OWN, 8, 128), F32),
        len(operands),
        (
            pltpu.VMEM((MB, 2 * KP), BF16),
            pltpu.VMEM((FR // 8, 8, NN), F32),
            pltpu.VMEM((FB, NN), F32),
            pltpu.VMEM((FB, NN), F32),
        ),
        smem=(0,),
    )(*operands)


def pack_call(body, rows, *operands):
    return call(
        body,
        jax.ShapeDtypeStruct((OWN, rows, 128), BF16),
        len(operands),
        (pltpu.VMEM((OWN * PAD, 128), F32),),
    )(*operands)


def ranks(frame_lens):
    ids = jnp.arange(GRP, dtype=jnp.int32)
    a, b = frame_lens[:, None], frame_lens[None, :]
    ahead = (a > b) | ((a == b) & (ids[:, None] < ids[None, :]))
    return jnp.sum(ahead.astype(jnp.int32), axis=0)[None, :]


def owned(lens, rank, own):
    slots = jnp.arange(GRP // OWN, dtype=jnp.int32) * OWN + own
    return jnp.sum(jnp.where(rank == slots[:, None], lens[None, :], 0), axis=1)


def lanes_of(lens):
    parts = jnp.repeat(lens.reshape(NCH, 1, NU), OWN, axis=2)
    return jnp.broadcast_to(parts, (NCH, 8, 128))


def counts_of(frame_own):
    longest = jnp.max(frame_own.reshape(NCH, NU), axis=1)
    return jnp.concatenate([(longest + MB - 1) // MB, (longest + 2 * FB - 1) // (2 * FB)])


def over_groups(x):
    x = x + lax.ppermute(x, "dp_1", [(0, 1), (1, 0)])
    turns = [lax.ppermute(x, "dp_0", [(i, (i + n) % 4) for i in range(4)]) for n in (1, 2, 3)]
    return x + turns[0] + turns[1] + turns[2]


def shards(means, log_scales, latents, text_lens, frame_lens):
    own = lax.axis_index(SEQ).astype(jnp.int32)
    rank = ranks(frame_lens)
    text_own, frame_own = owned(text_lens, rank, own), owned(frame_lens, rank, own)
    means, log_scales, latents = (jnp.transpose(x, (1, 2, 0)) for x in (means, log_scales, latents))
    first = exchange(pack_call(pack_first, 2 * PROWS + ROWS, rank, means, log_scales, latents))
    second = exchange(pack_call(pack_second, ROWS, rank, latents))
    text_lanes, frame_lanes, counts = lanes_of(text_own), lanes_of(frame_own), counts_of(frame_own)
    sides = (*make_rhs(first, text_lanes), text_lanes, frame_lanes)
    back = run_search(0, 2 * PROWS, counts, first, *sides)
    back = exchange(run_search(1, 0, counts, second, *sides, back))
    pos, sums = call(
        unpack,
        (jax.ShapeDtypeStruct((FB, GRP), F32), jax.ShapeDtypeStruct((8, 128), F32)),
        3,
        (pltpu.VMEM((128, 2 * 128), F32),),
    )(rank, frame_lens[None, :], back.reshape(OWN * 8, 128))
    sums = over_groups(sums)
    return (jnp.transpose(pos), -sums[0, 64] / sums[0, 0])


def solution(mesh):
    torus = Mesh(mesh.devices.reshape(4, 2, 4, 8), ("dp_0", "dp_1", "seq_0", "seq_1"))
    in_specs = (P(DP, SEQ, None), P(DP, SEQ, None), P(DP, SEQ, None), P(DP), P(DP))
    out_specs = (P(DP, SEQ), P())
    return jax.shard_map(
        shards, mesh=torus, in_specs=in_specs, out_specs=out_specs, check_vma=False
    )
```

time: 290 us -> 250 us (0.86)
  Pallas kernels: 108 us -> 81.1 us
  starting transfers between devices: 41.7 us -> 25.3 us
  waiting for transfers between devices: 106 us -> 116 us
  local copies, waits for them, and re-layouts: 7.8 us -> 3.7 us
  between operations: 6.49 us -> 3.11 us
  blocking collectives: 13.2 us -> 16.3 us
    pallas_call x7 -> x5, Pallas kernels: 106 us -> 79.2 us  [the longest x2 50.4 us: run_search(): call(functools.partial(search, chunk, first_row), jax.ShapeDtypeStruct((O...]
    all_to_all x5 -> x2, starting transfers between devices: 41.7 us -> 20 us  [exchange(): return lax.all_to_all(x, SEQ, split_axis=0, concat_axis=0, tiled=True)]
    all_to_all x0 -> x1, blocking collectives: none -> 16.3 us  [exchange(): return lax.all_to_all(x, SEQ, split_axis=0, concat_axis=0, tiled=True)]
    psum x1 -> x0, blocking collectives: 13.2 us -> none  [shards(): path_total = lax.psum(finish[0, 0], DP)]
    all_to_all x5 -> x2, waiting for transfers between devices: 106 us -> 112 us  [exchange(): return lax.all_to_all(x, SEQ, split_axis=0, concat_axis=0, tiled=True)]
    ppermute x0 -> x4, starting transfers between devices: none -> 5.37 us  [the longest x3 5.36 us: over_groups(): lax.ppermute(x, 'dp_0', [(i, (i + n) % 4) for i in range(4)])]
    ppermute x0 -> x4, waiting for transfers between devices: none -> 3.71 us  [the longest x3 2.34 us: over_groups(): lax.ppermute(x, 'dp_0', [(i, (i + n) % 4) for i in range(4)])]
  transfers between devices with their start and end apart: 5 -> 6, of which waited for: 4 -> 5; matrix products, arithmetic and copies ran while one was open for 2% -> 1% of each run, Pallas kernels for 31% -> 18%
where the time goes in v2:
time: 250 us; the launch traced here: 249 us
  waiting for transfers between devices  116 us (46%)
  Pallas kernels  81.1 us (32%)
  starting transfers between devices  25.3 us (10%)
  blocking collectives  16.3 us (7%)
  local copies, waits for them, and re-layouts  3.7 us (1%)
  between operations  3.11 us (1%)
  other arithmetic  3.05 us (1%)
    all_to_all x2, waiting for transfers between devices, exchange(): return lax.all_to_all(x, SEQ, split_axis=0, concat_axis=0, tiled=True)  112 us
    pallas_call x2, Pallas kernels, run_search(): call(functools.partial(search, chunk, first_row), jax.ShapeDtypeStruct((O...  50.4 us
    pallas_call x2, Pallas kernels, pack_call(): call(body, jax.ShapeDtypeStruct((OWN, rows, 128), BF16), len(operands), (...  20.4 us
    all_to_all x2, starting transfers between devices, exchange(): return lax.all_to_all(x, SEQ, split_axis=0, concat_axis=0, tiled=True)  20 us
    all_to_all x1, blocking collectives, exchange(): return lax.all_to_all(x, SEQ, split_axis=0, concat_axis=0, tiled=True)  16.3 us
    pallas_call x1, Pallas kernels, make_rhs(): call(build_sides, (jax.ShapeDtypeStruct((NCH * 2, KP, KP), BF16), jax.Sha...  8.41 us
    ppermute x3, starting transfers between devices, over_groups(): lax.ppermute(x, 'dp_0', [(i, (i + n) % 4) for i in range(4)])  5.36 us
  transfers between devices with their start and end apart: 6, of which 5 were waited for; matrix products, arithmetic and copies ran while one was open for 1% of the time, Pallas kernels for 18%

profile of v2, /device:TPU:32, one launch (start us, length us, event | category | flops | bytes accessed | tf_op | source)
XLA Modules:
  0.0 248.7 jit_solution(11514598193890431669)
XLA Ops:
  0.6 1.5 convert_reduce_fusion
  2.1 12.3 %shard_map.69 = bf16[32,576,128]{2,1,0:T(8,128)(2,1)} custom-call(s32[1,256]{1,0:T(1,128)} %bitcast.13, bf16[12,192,256]{2,1,0:T(8,128)(2,1)} %bitcast.10, bf16[12,192,256]{2,1,0:T(8,128)(2,1)} %bitcast.11, bf16[48,192,256]{2,1,0:T(8,128)(2,1)} %bitcast.8), custom_call_target="tpu_custom_call" | custom-call | tf_op jit(solution)/shard_map/pallas_call | solution.py:338
  14.4 11.2 %all-to-all-start.1 = ((bf16[32,576,128]{2,1,0:T(8,128)(2,1)}), bf16[32,576,128]{2,1,0:T(8,128)(2,1)}, u32[]{:S(2)}, u32[]{:S(2)}) async-start(bf16[32,576,128]{2,1,0:T(8,128)(2,1)} %shard_map.69), calls=%async_computation.1 | async-start | bytes 9437184 | tf_op jit(solution)/shard_map/all_to_all | solution.py:309
  25.6 8.1 %shard_map.68 = bf16[32,288,128]{2,1,0:T(8,128)(2,1)} custom-call(s32[1,256]{1,0:T(1,128)} %bitcast.14, bf16[48,192,256]{2,1,0:T(8,128)(2,1)} %bitcast.9), custom_call_target="tpu_custom_call" | custom-call | tf_op jit(solution)/shard_map/pallas_call | solution.py:338
  33.8 98.4 %all-to-all-done.1.y_ref = bf16[32,576,128]{2,1,0:T(8,128)(2,1)} async-done(((bf16[32,576,128]{2,1,0:T(8,128)(2,1)}), bf16[32,576,128]{2,1,0:T(8,128)(2,1)}, u32[]{:S(2)}, u32[]{:S(2)}) %all-to-all-start.1) | async-done | bytes 4718624 | tf_op jit(solution)/shard_map/all_to_all | solution.py:309
  132.1 8.7 %all-to-all-start = ((bf16[32,288,128]{2,1,0:T(8,128)(2,1)}), bf16[32,288,128]{2,1,0:T(8,128)(2,1)S(1)}, u32[]{:S(2)}, u32[]{:S(2)}) async-start(bf16[32,288,128]{2,1,0:T(8,128)(2,1)} %shard_map.68), calls=%async_computation | async-start | bytes 4718592 | tf_op jit(solution)/shard_map/all_to_all | solution.py:309
  141.7 0.6 pad_add_fusion.count_ref
  142.3 0.6 broadcast_in_dim.59.text_ref
  142.9 8.4 %shard_map.70 = (bf16[4,768,768]{2,1,0:T(8,128)(2,1)}, f32[2,8,1536]{2,1,0:T(8,128)}) custom-call(bf16[32,576,128]{2,1,0:T(8,128)(2,1)} %all-to-all-done.1.y_ref, s32[2,8,128]{2,1,0:T(8,128)} %broadcast_in_dim.59.text_ref), custom_call_target="tpu_custom_call" | custom-call | tf_op jit(solution)/shard_map/pallas_call | solution.py:314
  151.3 0.6 broadcast_in_dim.62.frame_ref
  151.9 29.2 %shard_map.71.rest_0_ = f32[32,8,128]{2,1,0:T(8,128)} custom-call(s32[4]{0:T(128)} %pad_add_fusion.count_ref, bf16[32,576,128]{2,1,0:T(8,128)(2,1)} %all-to-all-done.1.y_ref, bf16[4,768,768]{2,1,0:T(8,128)(2,1)} %get-tuple-element.6.rhs_ref, f32[2,8,1536]{2,1,0:T(8,128)} %get-tuple-element.7.bias_ref, s32[2,8,128]{2,1,0:T(8,128)} %broadcast_in_dim.59.text_ref, ...), custom_call_target="tpu_custom_call" | custom-call | tf_op jit(solution)/shard_map/pallas_call | solution.py:323
  181.1 14.1 %all-to-all-done.y_ref = bf16[32,288,128]{2,1,0:T(8,128)(2,1)S(1)} async-done(((bf16[32,288,128]{2,1,0:T(8,128)(2,1)}), bf16[32,288,128]{2,1,0:T(8,128)(2,1)S(1)}, u32[]{:S(2)}, u32[]{:S(2)}) %all-to-all-start) | async-done | bytes 2359328 | tf_op jit(solution)/shard_map/all_to_all | solution.py:309
  195.2 1.4 copy-done
  196.6 21.2 %shard_map.72 = f32[32,8,128]{2,1,0:T(8,128)} custom-call(s32[4]{0:T(128)} %pad_add_fusion.count_ref, bf16[32,288,128]{2,1,0:T(8,128)(2,1)} %copy-done, bf16[4,768,768]{2,1,0:T(8,128)(2,1)} %get-tuple-element.6.rhs_ref, f32[2,8,1536]{2,1,0:T(8,128)} %get-tuple-element.7.bias_ref, s32[2,8,128]{2,1,0:T(8,128)} %broadcast_in_dim.59.text_ref, ...), custom_call_target="tpu_custom_call" | custom-call | tf_op jit(solution)/shard_map/pallas_call | solution.py:323
  217.8 16.3 %all_to_all.15 = f32[32,8,128]{2,1,0:T(8,128)} all-to-all(f32[32,8,128]{2,1,0:T(8,128)} %shard_map.72), channel_id=1, replica_groups=mesh['dp_0'=4,'dp_1'=2,'seq_0'=4,'seq_1'=8] {'seq_0','seq_1'}, dimensions={0} | all-to-all | bytes 262144 | tf_op jit(solution)/shard_map/all_to_all | solution.py:309
  234.1 1.8 shard_map.73
  236.0 1.4 collective-permute-done
  237.4 0.7 add.40
  238.0 1.6 collective-permute-start.1
  239.6 2.5 %collective-permute-start.2 = (f32[8,128]{1,0:T(8,128)S(1)}, f32[8,128]{1,0:T(8,128)S(1)}, u32[]{:S(2)}, u32[]{:S(2)}) collective-permute-start(f32[8,128]{1,0:T(8,128)S(1)} %add.40), channel_id=1, source_target_pairs={{0,128},{64,192},{128,0},{192,64},{1,129},{65,193},{129,1},{193,65... | collective-permute-start | bytes 12296 | tf_op jit(solution)/shard_map/ppermute | solution.py:370
  242.1 1.3 collective-permute-start.3
  243.4 1.3 collective-permute-done.2
  244.7 1.0 collective-permute-done.3
  245.7 0.6 fusion.4
  (20 shorter events, 0.8 us)
Async XLA Ops:
  14.4 117.7 %all-to-all-start.1 = ((bf16[32,576,128]{2,1,0:T(8,128)(2,1)}), bf16[32,576,128]{2,1,0:T(8,128)(2,1)}, u32[]{:S(2)}, u32[]{:S(2)}) async-start(bf16[32,576,128]{2,1,0:T(8,128)(2,1)} %shard_map.69), calls=%async_computation.1 | async-start | bytes 9437184 | tf_op jit(solution)/shard_map/all_to_all | solution.py:309
  25.6 115.3 %copy-start.1 = (s32[256]{0:T(256)S(1)}, s32[256]{0:T(256)}, u32[]{:S(2)}) copy-start(s32[256]{0:T(256)} %convert_reduce_fusion) | copy-start | bytes 3076
  25.6 115.3 %copy-start.2 = (s32[256]{0:T(256)S(1)}, s32[256]{0:T(256)}, u32[]{:S(2)}) copy-start(s32[256]{0:T(256)} %param.9) | copy-start | bytes 3076
  25.6 115.3 %copy-start.3 = (s32[256]{0:T(256)S(1)}, s32[256]{0:T(256)}, u32[]{:S(2)}) copy-start(s32[256]{0:T(256)} %param.8) | copy-start | bytes 3076
  132.1 63.0 %all-to-all-start = ((bf16[32,288,128]{2,1,0:T(8,128)(2,1)}), bf16[32,288,128]{2,1,0:T(8,128)(2,1)S(1)}, u32[]{:S(2)}, u32[]{:S(2)}) async-start(bf16[32,288,128]{2,1,0:T(8,128)(2,1)} %shard_map.68), calls=%async_computation | async-start | bytes 4718592 | tf_op jit(solution)/shard_map/all_to_all | solution.py:309
  195.2 1.4 copy-start
  236.0 1.4 collective-permute-start
  238.0 5.4 %collective-permute-start.1 = (f32[8,128]{1,0:T(8,128)S(1)}, f32[8,128]{1,0:T(8,128)S(1)}, u32[]{:S(2)}, u32[]{:S(2)}) collective-permute-start(f32[8,128]{1,0:T(8,128)S(1)} %add.40), channel_id=1, source_target_pairs={{0,64},{64,128},{128,192},{192,0},{1,65},{65,129},{129,193},{193,1... | collective-permute-start | bytes 12296 | tf_op jit(solution)/shard_map/ppermute | solution.py:370
  239.6 5.1 %collective-permute-start.2 = (f32[8,128]{1,0:T(8,128)S(1)}, f32[8,128]{1,0:T(8,128)S(1)}, u32[]{:S(2)}, u32[]{:S(2)}) collective-permute-start(f32[8,128]{1,0:T(8,128)S(1)} %add.40), channel_id=1, source_target_pairs={{0,128},{64,192},{128,0},{192,64},{1,129},{65,193},{129,1},{193,65... | collective-permute-start | bytes 12296 | tf_op jit(solution)/shard_map/ppermute | solution.py:370
  242.1 3.6 %collective-permute-start.3 = (f32[8,128]{1,0:T(8,128)S(1)}, f32[8,128]{1,0:T(8,128)S(1)}, u32[]{:S(2)}, u32[]{:S(2)}) collective-permute-start(f32[8,128]{1,0:T(8,128)S(1)} %add.40), channel_id=1, source_target_pairs={{0,192},{64,0},{128,64},{192,128},{1,193},{65,1},{129,65},{193,129... | collective-permute-start | bytes 12296 | tf_op jit(solution)/shard_map/ppermute | solution.py:370

commit v3 on v2

--- a/solution.py
+++ b/solution.py
@@ -25,7 +25,8 @@
 PROWS = (GRP // OWN) * 3 // 2 * TB
 PAD = 296
 KP = 2 * 3 * 128
-UNROLL = 4
+FRAME_UNROLL = 16
+TOKEN_UNROLL = 6
 NN = TB * 128
 MB = 384
 
@@ -37,11 +38,7 @@
 NN_DIMS = (((1,), (0,)), ((), ()))
 
 
-def params():
-    return pltpu.CompilerParams(vmem_limit_bytes=60 * 1024 * 1024)
-
-
-def call(body, out_shape, n_in, scratch=(), smem=()):
+def call(body, out_shape, n_in, scratch=(), smem=(), mib=24):
     vmem = pl.BlockSpec(memory_space=pltpu.VMEM)
     return pl.pallas_call(
         body,
@@ -49,7 +46,7 @@
         in_specs=[pl.BlockSpec(memory_space=pltpu.SMEM) if i in smem else vmem for i in range(n_in)],
         out_specs=jax.tree.map(lambda _: vmem, out_shape),
         scratch_shapes=list(scratch),
-        compiler_params=params(),
+        compiler_params=pltpu.CompilerParams(vmem_limit_bytes=mib * 1024 * 1024),
     )
 
 
@@ -68,36 +65,31 @@
         stage[pl.ds(pair_at + p * step, OWN, stride=PAD), :] = jnp.concatenate([low, high], axis=1)
 
 
-def unstage(stage, out_ref, rows):
-    for d in range(OWN):
-        out_ref[d] = stage[d * PAD : d * PAD + rows, :].astype(BF16)
-
-
 def stage_priors(rank_ref, means_ref, logs_ref, stage):
     picks = one_hot(rank_ref[...], 0, GRP, BF16)
     count = GRP // OWN
 
     def tokens(i, _):
-        for q in range(UNROLL // 2):
+        for q in range(TOKEN_UNROLL):
             for which, ref in enumerate((means_ref, logs_ref)):
-                token = i * (UNROLL // 2) + q
+                token = i * TOKEN_UNROLL + q
                 at = which * PROWS + token
                 pack_block(ref[token], picks, stage, at, at + count * TB, TB, count)
         return 0
 
-    lax.fori_loop(0, 2 * TB // UNROLL, tokens, 0)
+    lax.fori_loop(0, TB // TOKEN_UNROLL, tokens, 0)
 
 
 def stage_latents(chunk, rank_ref, lat_ref, stage):
     picks = one_hot(rank_ref[...], chunk * NU * OWN, NU * OWN, BF16)
 
     def frames(j, _):
-        for q in range(UNROLL):
-            frame = j * UNROLL + q
+        for q in range(FRAME_UNROLL):
+            frame = j * FRAME_UNROLL + q
             pack_block(lat_ref[frame], picks, stage, frame, frame + NU * FB, FB, NU)
         return 0
 
-    lax.fori_loop(0, FB // UNROLL, frames, 0)
+    lax.fori_loop(0, FB // FRAME_UNROLL, frames, 0)
 
 
 def unstage(stage, out_ref, first, rows):
@@ -117,7 +109,7 @@
     unstage(stage, out_ref, 0, ROWS)
 
 
-def build_sides(y_ref, text_ref, rhs_ref, bias_ref, wt, pr, zz, zs):
+def build_sides(y_ref, text_ref, rhs0_ref, rhs1_ref, bias0_ref, bias1_ref, wt, pr, zz, zs):
     wide = 152
     for s in range(OWN):
         m = y_ref[s, 0:PROWS, :].astype(F32)
@@ -151,7 +143,7 @@
                 for q, pieces in enumerate((first, second, mixed)):
                     turned = jnp.concatenate(pieces, axis=0).T.astype(BF16)
                     k = (half * 3 + q) * 128
-                    rhs_ref[pair, k : k + 128, v * 128 : (v + 1) * 128] = turned * jnp.asarray(factor, BF16)
+                    (rhs0_ref, rhs1_ref)[c][p, k : k + 128, v * 128 : (v + 1) * 128] = turned * jnp.asarray(factor, BF16)
         for i in range(TB):
             for k, extra in enumerate(both(zz, pair, i)):
                 at = c * NN + i * 128 + (2 * p + k) * OWN
@@ -167,7 +159,7 @@
                 preferred_element_type=F32,
             )
             token = (lane8 % OWN) * TB + i
-            bias_ref[c, :, i * 128 : (i + 1) * 128] = jnp.where(
+            (bias0_ref, bias1_ref)[c][:, i * 128 : (i + 1) * 128] = jnp.where(
                 token < text, -total - C * HALF_LOG_TWO_PI, NEG
             )
 
@@ -194,7 +186,7 @@
             got = [
                 lax.dot_general(
                     lhs[:, p * KP : (p + 1) * KP],
-                    rhs_ref[chunk * 2 + p, :, t * 256 : (t + 1) * 256],
+                    rhs_ref[p, :, t * 256 : (t + 1) * 256],
                     NN_DIMS,
                     preferred_element_type=F32,
                 )
@@ -207,7 +199,7 @@
                 odd = jnp.where(wide_lane < 64, pltpu.roll(one, 64, 1), two)
                 for n, x in enumerate((even, odd)):
                     cols = slice((i + n) * 128, (i + n + 1) * 128)
-                    lik[group, :, cols] = (x + bias_ref[chunk, 0:1, cols]).reshape(MB // 8, 8, 128)
+                    lik[group, :, cols] = (x + bias_ref[0:1, cols]).reshape(MB // 8, 8, 128)
         return 0
 
     lax.fori_loop(0, count_ref[chunk], matmul_block, 0)
@@ -245,11 +237,23 @@
             out = jnp.broadcast_to(one, (8, 128)) if out is None else jnp.where(seg == k, one, out)
         return out
 
+    seg_rows = lax.broadcasted_iota(jnp.int32, (128, 128), 0) // OWN
+    seg_cols = lax.broadcasted_iota(jnp.int32, (128, 128), 1) // OWN
+    same = jnp.where(seg_rows == seg_cols, 1.0, 0.0).astype(BF16)
+
+    def over_segment(x):
+        high = x.astype(BF16)
+        rest = x - high.astype(F32)
+        mid = rest.astype(BF16)
+        low = (rest - mid.astype(F32)).astype(BF16)
+        parts = [lax.dot_general(y, same, NN_DIMS, preferred_element_type=F32) for y in (high, mid, low)]
+        return parts[0] + (parts[1] + parts[2])
+
     def soften(index, buf, finish):
-        rows = []
+        frame = index * FB + lax.broadcasted_iota(jnp.int32, (FB, 128), 0)
+        weights, moments, tops = [], [], []
         for g in range(FB // 8):
-            frame = index * FB + g * 8 + sub
-            late = frame - base
+            late = index * FB + g * 8 + sub - base
             xs = [
                 jnp.where(late <= i, buf[g * 8 : (g + 1) * 8, i * 128 : (i + 1) * 128], 8 * NEG)
                 for i in range(TB)
@@ -262,11 +266,14 @@
                 suffix = suffix + ws[i]
                 moment = moment + suffix
             weight = suffix + ws[0]
-            moment = moment + block_start * weight
-            weight = by_segment(weight, jnp.sum, 0.0)
-            moment = by_segment(moment, jnp.sum, 0.0)
-            rows.append(jnp.where(frame < frames, moment / weight * inverse, 0.0))
-            finish = finish + jnp.where(frame == frames - 1, top, 0.0)
+            weights.append(weight)
+            moments.append(moment + block_start * weight)
+            tops.append(top)
+        weight, moment = (over_segment(jnp.concatenate(x, axis=0)) for x in (weights, moments))
+        place = jnp.where(frame < frames[0:1], moment / weight * inverse[0:1], 0.0)
+        ended = jnp.where(frame == frames[0:1] - 1, jnp.concatenate(tops, axis=0), 0.0)
+        finish = finish + jnp.sum(ended.reshape(FB // 8, 8, 128), axis=0)
+        rows = [place]
         turned = jnp.concatenate(rows + [jnp.zeros((128 - FB, 128), F32)], axis=0).T
         where = jnp.maximum(index, 0)
         for k in range(NU):
@@ -290,19 +297,21 @@
         out_ref[d, chunk * NU : chunk * NU + 1, 64:128] = jnp.broadcast_to(finish, (1, 64))
 
 
-def unpack(rank_ref, frame_ref, got_ref, pos_ref, sums_ref, turned):
-    lane1 = lax.broadcasted_iota(jnp.int32, (1, 128), 1)
+def unpack(rank_ref, got_ref, pos_ref, turned):
     rows = [got_ref[pl.ds(k, OWN, stride=8), :] for k in range(NCH * NU)]
-    finish = sum(jnp.sum(rows[c * NU], axis=0, keepdims=True) for c in range(NCH))
     for c in range(2):
         turned[:, c * 128 : (c + 1) * 128] = jnp.concatenate(rows[c * 4 : c * 4 + 4], axis=0).T
     picks = one_hot(rank_ref[...], 0, GRP, F32)
     pos_ref[...] = lax.dot_general(
         turned[0:FB, :], picks, NN_DIMS, precision=lax.Precision.HIGHEST, preferred_element_type=F32
     )
-    lens = jnp.sum(frame_ref[...].astype(F32), axis=1, keepdims=True)
-    sums = jnp.where(lane1 >= 64, finish, lens)
-    sums_ref[...] = jnp.broadcast_to(sums, (8, 128))
+
+
+def sum_up(back, frame_lens):
+    finish = jnp.sum(back, axis=(0, 1), keepdims=True)[0]
+    lens = jnp.sum(frame_lens).astype(F32)
+    lanes = lax.broadcasted_iota(jnp.int32, (1, 128), 1)
+    return jnp.where(lanes >= 64, finish, lens)
 
 
 def exchange(x):
@@ -313,9 +322,10 @@
     wide = pltpu.VMEM((OWN * 152, 128), F32)
     return call(
         build_sides,
-        (jax.ShapeDtypeStruct((NCH * 2, KP, KP), BF16), jax.ShapeDtypeStruct((NCH, 8, NN), F32)),
+        (jax.ShapeDtypeStruct((2, KP, KP), BF16),) * NCH + (jax.ShapeDtypeStruct((8, NN), F32),) * NCH,
         2,
         (wide, wide, wide, pltpu.VMEM((NCH * NN, 128), F32)),
+        mib=32,
     )(first, text_lanes)
 
 
@@ -367,8 +377,9 @@
 
 def over_groups(x):
     x = x + lax.ppermute(x, "dp_1", [(0, 1), (1, 0)])
-    turns = [lax.ppermute(x, "dp_0", [(i, (i + n) % 4) for i in range(4)]) for n in (1, 2, 3)]
-    return x + turns[0] + turns[1] + turns[2]
+    for n in (1, 2):
+        x = x + lax.ppermute(x, "dp_0", [(i, (i + n) % 4) for i in range(4)])
+    return x
 
 
 def shards(means, log_scales, latents, text_lens, frame_lens):
@@ -379,16 +390,13 @@
     first = exchange(pack_call(pack_first, 2 * PROWS + ROWS, rank, means, log_scales, latents))
     second = exchange(pack_call(pack_second, ROWS, rank, latents))
     text_lanes, frame_lanes, counts = lanes_of(text_own), lanes_of(frame_own), counts_of(frame_own)
-    sides = (*make_rhs(first, text_lanes), text_lanes, frame_lanes)
-    back = run_search(0, 2 * PROWS, counts, first, *sides)
-    back = exchange(run_search(1, 0, counts, second, *sides, back))
-    pos, sums = call(
-        unpack,
-        (jax.ShapeDtypeStruct((FB, GRP), F32), jax.ShapeDtypeStruct((8, 128), F32)),
-        3,
-        (pltpu.VMEM((128, 2 * 128), F32),),
-    )(rank, frame_lens[None, :], back.reshape(OWN * 8, 128))
-    sums = over_groups(sums)
+    rhs0, rhs1, bias0, bias1 = make_rhs(first, text_lanes)
+    back = run_search(0, 2 * PROWS, counts, first, rhs0, bias0, text_lanes, frame_lanes)
+    back = exchange(run_search(1, 0, counts, second, rhs1, bias1, text_lanes, frame_lanes, back))
+    sums = over_groups(sum_up(back, frame_lens))
+    pos = call(
+        unpack, jax.ShapeDtypeStruct((FB, GRP), F32), 2, (pltpu.VMEM((128, 2 * 128), F32),)
+    )(rank, back.reshape(OWN * 8, 128))
     return (jnp.transpose(pos), -sums[0, 64] / sums[0, 0])
 
 

time: 250 us -> 242 us (0.968)
  Pallas kernels: 81.1 us -> 52.1 us
  waiting for transfers between devices: 116 us -> 137 us
  blocking collectives: 16.3 us -> 0 us
  local copies, waits for them, and re-layouts: 3.7 us -> 14.9 us
  starting transfers between devices: 25.3 us -> 31.4 us
    all_to_all x2 -> x3, waiting for transfers between devices: 112 us -> 131 us  [exchange(): return lax.all_to_all(x, SEQ, split_axis=0, concat_axis=0, tiled=True)]
    all_to_all x1 -> x0, blocking collectives: 16.3 us -> none  [exchange(): return lax.all_to_all(x, SEQ, split_axis=0, concat_axis=0, tiled=True)]
    pallas_call x2, Pallas kernels: 20.4 us -> 6.79 us  [pack_call(): call(body, jax.ShapeDtypeStruct((OWN, rows, 128), BF16), len(operands), (...]
    unnamed x8 -> x20, local copies, waits for them, and re-layouts: 1.45 us -> 13.8 us
    pallas_call x2, Pallas kernels: 50.4 us -> 38.1 us  [run_search(): call(functools.partial(search, chunk, first_row), jax.ShapeDtypeStruct((O...]
    all_to_all x2 -> x3, starting transfers between devices: 20 us -> 26.6 us  [exchange(): return lax.all_to_all(x, SEQ, split_axis=0, concat_axis=0, tiled=True)]
    pallas_call x2, Pallas kernels: 10.3 us -> 7.17 us  [the longest x1 6.25 us: make_rhs(): call(build_sides, (jax.ShapeDtypeStruct((2, KP, KP), BF16),) * NCH + (jax...]
    ppermute x3 -> x2, waiting for transfers between devices: 2.34 us -> 5.06 us  [over_groups(): x = x + lax.ppermute(x, 'dp_0', [(i, (i + n) % 4) for i in range(4)])]
  transfers between devices with their start and end apart: 6 -> 6, of which waited for: 5 -> 6; matrix products, arithmetic and copies ran while one was open for 1% -> 1% of each run, Pallas kernels for 18% -> 14%
where the time goes in v3:
time: 242 us; the launch traced here: 241 us
  waiting for transfers between devices  137 us (57%)
  Pallas kernels  52.1 us (22%)
  starting transfers between devices  31.4 us (13%)
  local copies, waits for them, and re-layouts  14.9 us (6%)
  between operations  3.82 us (2%)
    all_to_all x3, waiting for transfers between devices, exchange(): return lax.all_to_all(x, SEQ, split_axis=0, concat_axis=0, tiled=True)  131 us
    pallas_call x2, Pallas kernels, run_search(): call(functools.partial(search, chunk, first_row), jax.ShapeDtypeStruct((O...  38.1 us
    all_to_all x3, starting transfers between devices, exchange(): return lax.all_to_all(x, SEQ, split_axis=0, concat_axis=0, tiled=True)  26.6 us
    unnamed x20, local copies, waits for them, and re-layouts  13.8 us
    pallas_call x2, Pallas kernels, pack_call(): call(body, jax.ShapeDtypeStruct((OWN, rows, 128), BF16), len(operands), (...  6.79 us
    pallas_call x1, Pallas kernels, make_rhs(): call(build_sides, (jax.ShapeDtypeStruct((2, KP, KP), BF16),) * NCH + (jax...  6.25 us
    ppermute x2, waiting for transfers between devices, over_groups(): x = x + lax.ppermute(x, 'dp_0', [(i, (i + n) % 4) for i in range(4)])  5.06 us
  transfers between devices with their start and end apart: 6, of which 6 were waited for; matrix products, arithmetic and copies ran while one was open for 1% of the time, Pallas kernels for 14%

profile of v3, /device:TPU:32, one launch (start us, length us, event | category | flops | bytes accessed | tf_op | source)
XLA Modules:
  0.0 241.4 jit_solution(4264937309822876414)
XLA Ops:
  1.5 2.3 copy-done
  3.9 1.3 copy-done.6
  5.1 1.3 copy-done.7
  6.4 4.3 %shard_map.69 = bf16[32,576,128]{2,1,0:T(8,128)(2,1)S(1)} custom-call(s32[1,256]{1,0:T(1,128)S(1)} %bitcast.16, bf16[12,192,256]{2,1,0:T(8,128)(2,1)S(1)} %bitcast.13, bf16[12,192,256]{2,1,0:T(8,128)(2,1)S(1)} %bitcast.14, bf16[48,192,256]{2,1,0:T(8,128)(2,1)S(1)} %bitcast.11), custom_call_target="tpu_custom_call" | custom-call | tf_op jit(solution)/shard_map/pallas_call | solution.py:348
  10.7 2.1 copy-done.2
  12.8 11.2 %all-to-all-start.1 = ((bf16[32,576,128]{2,1,0:T(8,128)(2,1)}), bf16[32,576,128]{2,1,0:T(8,128)(2,1)}, u32[]{:S(2)}, u32[]{:S(2)}) async-start(bf16[32,576,128]{2,1,0:T(8,128)(2,1)} %copy-done.2), calls=%async_computation.1 | async-start | bytes 9437184 | tf_op jit(solution)/shard_map/all_to_all | solution.py:318
  24.1 2.3 copy-done.1
  26.4 2.5 %shard_map.68 = bf16[32,288,128]{2,1,0:T(8,128)(2,1)S(1)} custom-call(s32[1,256]{1,0:T(1,128)S(1)} %bitcast.17, bf16[48,192,256]{2,1,0:T(8,128)(2,1)S(1)} %bitcast.12), custom_call_target="tpu_custom_call" | custom-call | tf_op jit(solution)/shard_map/pallas_call | solution.py:348
  28.9 1.4 copy-done.3
  30.3 100.1 %all-to-all-done.1.y_ref = bf16[32,576,128]{2,1,0:T(8,128)(2,1)} async-done(((bf16[32,576,128]{2,1,0:T(8,128)(2,1)}), bf16[32,576,128]{2,1,0:T(8,128)(2,1)}, u32[]{:S(2)}, u32[]{:S(2)}) %all-to-all-start.1) | async-done | bytes 4718624 | tf_op jit(solution)/shard_map/all_to_all | solution.py:318
  130.4 8.7 %all-to-all-start = ((bf16[32,288,128]{2,1,0:T(8,128)(2,1)}), bf16[32,288,128]{2,1,0:T(8,128)(2,1)S(1)}, u32[]{:S(2)}, u32[]{:S(2)}) async-start(bf16[32,288,128]{2,1,0:T(8,128)(2,1)} %copy-done.3), calls=%async_computation | async-start | bytes 4718592 | tf_op jit(solution)/shard_map/all_to_all | solution.py:318
  140.0 6.3 %shard_map.70 = (bf16[2,768,768]{2,1,0:T(8,128)(2,1)S(1)}, bf16[2,768,768]{2,1,0:T(8,128)(2,1)S(1)}, f32[8,1536]{1,0:T(8,128)S(1)}, f32[8,1536]{1,0:T(8,128)S(1)}) custom-call(bf16[32,576,128]{2,1,0:T(8,128)(2,1)} %all-to-all-done.1.y_ref, s32[2,8,128]{2,1,0:T(8,128)S(1)} %broadcast_in_dim.59.text_ref), custom_call_target="tpu_custom_call" | custom-call | tf_op jit(solution)/shard_map/pallas_call | solution.py:323
  146.3 1.4 copy-done.4
  147.7 23.1 %shard_map.71.rest_0_ = f32[32,8,128]{2,1,0:T(8,128)S(1)} custom-call(s32[4]{0:T(128)S(1)} %pad_add_fusion.count_ref, bf16[32,576,128]{2,1,0:T(8,128)(2,1)} %all-to-all-done.1.y_ref, bf16[2,768,768]{2,1,0:T(8,128)(2,1)S(1)} %get-tuple-element.8.rhs_ref, f32[8,1536]{1,0:T(8,128)S(1)} %get-tuple-element.9.bias_ref, ...), custom_call_target="tpu_custom_call" | custom-call | tf_op jit(solution)/shard_map/pallas_call | solution.py:333
  170.9 22.6 %all-to-all-done.y_ref = bf16[32,288,128]{2,1,0:T(8,128)(2,1)S(1)} async-done(((bf16[32,288,128]{2,1,0:T(8,128)(2,1)}), bf16[32,288,128]{2,1,0:T(8,128)(2,1)S(1)}, u32[]{:S(2)}, u32[]{:S(2)}) %all-to-all-start) | async-done | bytes 2359328 | tf_op jit(solution)/shard_map/all_to_all | solution.py:318
  193.4 1.7 copy-done.5
  195.1 15.0 %shard_map.72 = f32[32,8,128]{2,1,0:T(8,128)} custom-call(s32[4]{0:T(128)S(1)} %pad_add_fusion.count_ref, bf16[32,288,128]{2,1,0:T(8,128)(2,1)S(1)} %all-to-all-done.y_ref, bf16[2,768,768]{2,1,0:T(8,128)(2,1)S(1)} %copy-done.5, f32[8,1536]{1,0:T(8,128)S(1)} %get-tuple-element.7.bias_ref, s32[2,8,128]{2,1,0:T(8,128)S(1)} %broadcast_in_dim.59.text_ref, ...), custom_call_target="tpu_custom_call" | custom-call | tf_op jit(solution)/shard_map/pallas_call | solution.py:333
  210.1 6.7 %all-to-all-start.2 = ((f32[32,8,128]{2,1,0:T(8,128)}), f32[32,8,128]{2,1,0:T(8,128)S(1)}, u32[]{:S(2)}, u32[]{:S(2)}) async-start(f32[32,8,128]{2,1,0:T(8,128)} %shard_map.72), calls=%async_computation.2 | async-start | bytes 262144 | tf_op jit(solution)/shard_map/all_to_all | solution.py:318
  218.0 8.4 %all-to-all-done.2 = f32[32,8,128]{2,1,0:T(8,128)S(1)} async-done(((f32[32,8,128]{2,1,0:T(8,128)}), f32[32,8,128]{2,1,0:T(8,128)S(1)}, u32[]{:S(2)}, u32[]{:S(2)}) %all-to-all-start.2) | async-done | bytes 131104 | tf_op jit(solution)/shard_map/all_to_all | solution.py:318
  226.6 1.1 collective-permute-done
  227.7 2.6 %collective-permute-start.1 = (f32[1,128]{1,0:T(1,128)S(1)}, f32[1,128]{1,0:T(1,128)S(1)}, u32[]{:S(2)}, u32[]{:S(2)}) collective-permute-start(f32[1,128]{1,0:T(1,128)S(1)} %fusion.5), channel_id=1, source_target_pairs={{0,64},{64,128},{128,192},{192,0},{1,65},{65,129},{129,193},{193,1... | collective-permute-start | bytes 1544 | tf_op jit(solution)/shard_map/ppermute | solution.py:381
  230.3 3.1 %collective-permute-done.1 = f32[1,128]{1,0:T(1,128)S(1)} collective-permute-done((f32[1,128]{1,0:T(1,128)S(1)}, f32[1,128]{1,0:T(1,128)S(1)}, u32[]{:S(2)}, u32[]{:S(2)}) %collective-permute-start.1) | collective-permute-done | bytes 544 | tf_op jit(solution)/shard_map/ppermute | solution.py:381
  233.4 2.2 collective-permute-start.2
  236.4 2.0 collective-permute-done.2
  (35 shorter events, 4.1 us)
Async XLA Ops:
  1.5 2.3 copy-start
  3.9 1.3 copy-start.6
  5.1 1.3 copy-start.7
  10.7 2.2 copy-start.2
  12.8 117.6 %all-to-all-start.1 = ((bf16[32,576,128]{2,1,0:T(8,128)(2,1)}), bf16[32,576,128]{2,1,0:T(8,128)(2,1)}, u32[]{:S(2)}, u32[]{:S(2)}) async-start(bf16[32,576,128]{2,1,0:T(8,128)(2,1)} %copy-done.2), calls=%async_computation.1 | async-start | bytes 9437184 | tf_op jit(solution)/shard_map/all_to_all | solution.py:318
  24.0 2.3 copy-start.1
  28.9 1.4 copy-start.3
  30.3 108.8 %copy-start.8 = (s32[256]{0:T(256)S(1)}, s32[256]{0:T(256)}, u32[]{:S(2)}) copy-start(s32[256]{0:T(256)} %param.9) | copy-start | bytes 3076
  30.3 108.8 %copy-start.9 = (s32[256]{0:T(256)S(1)}, s32[256]{0:T(256)}, u32[]{:S(2)}) copy-start(s32[256]{0:T(256)} %param.8) | copy-start | bytes 3076
  130.4 63.0 %all-to-all-start = ((bf16[32,288,128]{2,1,0:T(8,128)(2,1)}), bf16[32,288,128]{2,1,0:T(8,128)(2,1)S(1)}, u32[]{:S(2)}, u32[]{:S(2)}) async-start(bf16[32,288,128]{2,1,0:T(8,128)(2,1)} %copy-done.3), calls=%async_computation | async-start | bytes 4718592 | tf_op jit(solution)/shard_map/all_to_all | solution.py:318
  146.3 1.4 copy-start.4
  193.4 1.7 copy-start.5
  210.1 16.3 %all-to-all-start.2 = ((f32[32,8,128]{2,1,0:T(8,128)}), f32[32,8,128]{2,1,0:T(8,128)S(1)}, u32[]{:S(2)}, u32[]{:S(2)}) async-start(f32[32,8,128]{2,1,0:T(8,128)} %shard_map.72), calls=%async_computation.2 | async-start | bytes 262144 | tf_op jit(solution)/shard_map/all_to_all | solution.py:318
  226.5 1.2 collective-permute-start
  227.7 5.6 %collective-permute-start.1 = (f32[1,128]{1,0:T(1,128)S(1)}, f32[1,128]{1,0:T(1,128)S(1)}, u32[]{:S(2)}, u32[]{:S(2)}) collective-permute-start(f32[1,128]{1,0:T(1,128)S(1)} %fusion.5), channel_id=1, source_target_pairs={{0,64},{64,128},{128,192},{192,0},{1,65},{65,129},{129,193},{193,1... | collective-permute-start | bytes 1544 | tf_op jit(solution)/shard_map/ppermute | solution.py:381
  233.4 5.1 %collective-permute-start.2 = (f32[1,128]{1,0:T(1,128)S(1)}, f32[1,128]{1,0:T(1,128)S(1)}, u32[]{:S(2)}, u32[]{:S(2)}) collective-permute-start(f32[1,128]{1,0:T(1,128)S(1)} %add.38), channel_id=1, source_target_pairs={{0,128},{64,192},{128,0},{192,64},{1,129},{65,193},{129,1},{193,65... | collective-permute-start | bytes 1544 | tf_op jit(solution)/shard_map/ppermute | solution.py:381

commit v4 on v3

--- a/solution.py
+++ b/solution.py
@@ -23,6 +23,8 @@
 NCH = GRP // OWN // NU
 ROWS = (NU + NU // 2) * FB
 PROWS = (GRP // OWN) * 3 // 2 * TB
+CUT = 224
+LONG = FR - FR // 4
 PAD = 296
 KP = 2 * 3 * 128
 FRAME_UNROLL = 16
@@ -38,12 +40,15 @@
 NN_DIMS = (((1,), (0,)), ((), ()))
 
 
-def call(body, out_shape, n_in, scratch=(), smem=(), mib=24):
+def call(body, out_shape, n_in, scratch=(), smem=(), hbm=(), mib=24):
     vmem = pl.BlockSpec(memory_space=pltpu.VMEM)
     return pl.pallas_call(
         body,
         out_shape=out_shape,
-        in_specs=[pl.BlockSpec(memory_space=pltpu.SMEM) if i in smem else vmem for i in range(n_in)],
+        in_specs=[
+            pl.BlockSpec(memory_space=pltpu.SMEM if i in smem else pl.ANY if i in hbm else pltpu.VMEM)
+            for i in range(n_in)
+        ],
         out_specs=jax.tree.map(lambda _: vmem, out_shape),
         scratch_shapes=list(scratch),
         compiler_params=pltpu.CompilerParams(vmem_limit_bytes=mib * 1024 * 1024),
@@ -165,22 +170,40 @@
 
 
 def search(chunk, first_row, count_ref, y_ref, rhs_ref, bias_ref, text_ref, frame_ref, *rest):
-    earlier, (out_ref, lhs, lik, buf0, buf1) = rest[:-5], rest[-5:]
-    out_ref[...] = earlier[0][...] if earlier else jnp.zeros(out_ref.shape, F32)
+    if chunk == 0:
+        out_ref, lhs, lik, buf0, buf1 = rest
+        out_ref[...] = jnp.zeros(out_ref.shape, F32)
+    else:
+        earlier_ref, far_ref, out_ref, lhs, lik, buf0, buf1, far, sem = rest
+        out_ref[...] = earlier_ref[...]
     per = MB // FB
     wide_lane = lax.broadcasted_iota(jnp.int32, (MB, 128), 1)
 
-    def matmul_block(b, _):
+    def pieces_of(b, q, k):
+        if chunk == 0:
+            return ((y_ref, b * per + q, first_row + k * FB, FB),)
+        own = max(0, min(FB, CUT - k * FB))
+        parts = ((y_ref, b * per + q, k * FB, own),)
+        rest = pl.multiple_of(b * (ROWS - CUT) + (k * FB + own - CUT), 16) if own < FB else 0
+        return parts + ((y_ref, 3 * per + q, rest, FB - own),)
+
+    def far_pieces(b, q, k):
+        return ((far, q, k * FB, FB),)
+
+    def matmul_block(b, _, pieces=pieces_of):
         for q in range(per):
-            s = b * per + q
-            rows = slice(q * FB, (q + 1) * FB)
             for p in range(NU // 2):
                 for n, k in enumerate((2 * p, 2 * p + 1, NU + p)):
-                    x = y_ref[s, first_row + k * FB : first_row + (k + 1) * FB, :]
                     at = p * KP + n * 128
-                    lhs[rows, at : at + 128] = x
-                    wide = x.astype(F32)
-                    lhs[rows, at + 384 : at + 512] = (wide * wide).astype(BF16)
+                    done = q * FB
+                    for ref, s, row, rows in pieces(b, q, k):
+                        if not rows:
+                            continue
+                        x = ref[s, pl.ds(row, rows), :]
+                        lhs[done : done + rows, at : at + 128] = x
+                        wide = x.astype(F32)
+                        lhs[done : done + rows, at + 384 : at + 512] = (wide * wide).astype(BF16)
+                        done += rows
         group = pl.ds(b * (MB // 8), MB // 8)
         for t in range(KP // 256):
             got = [
@@ -202,7 +225,17 @@
                     lik[group, :, cols] = (x + bias_ref[0:1, cols]).reshape(MB // 8, 8, 128)
         return 0
 
-    lax.fori_loop(0, count_ref[chunk], matmul_block, 0)
+    if chunk == 0:
+        lax.fori_loop(0, count_ref[chunk], matmul_block, 0)
+    else:
+        lax.fori_loop(0, jnp.minimum(count_ref[chunk], 3), matmul_block, 0)
+
+        @pl.when(count_ref[chunk] > 3)
+        def _():
+            copy = pltpu.make_async_copy(far_ref, far, sem)
+            copy.start()
+            copy.wait()
+            matmul_block(3, 0, far_pieces)
 
     lane = lax.broadcasted_iota(jnp.int32, (8, 128), 1)
     sub = lax.broadcasted_iota(jnp.int32, (8, 128), 0)
@@ -318,6 +351,28 @@
     return lax.all_to_all(x, SEQ, split_axis=0, concat_axis=0, tiled=True)
 
 
+def over_dp(x, combine):
+    x = combine(x, lax.ppermute(x, "dp_1", [(0, 1), (1, 0)]))
+    for n in (1, 2):
+        x = combine(x, lax.ppermute(x, "dp_0", [(i, (i + n) % 4) for i in range(4)]))
+    return x
+
+
+def exchange_short(first, x, rank, frame_lens):
+    relayed = [lax.ppermute(x[:, CUT:], "seq_0", [(i, 3)]) for i in range(3)]
+    relayed = jnp.concatenate([*relayed, x[:, : CUT - 3 * (ROWS - CUT)]], axis=1)
+    send = jnp.where(lax.axis_index("seq_0") == 3, relayed, x[:, :CUT])
+    first, send = lax.optimization_barrier((first, send))
+    got = exchange(send)
+    longest = jnp.max(jnp.where(rank[0] >= NU * OWN, frame_lens, 0)).astype(F32)
+    longest = over_dp(jnp.full((1, 128), longest), jnp.maximum)[0, 0]
+    last = slice(3 * OWN // 4, OWN)
+    got, longest = lax.optimization_barrier((got, longest))
+    none = lambda v: jnp.zeros((OWN // 4, ROWS, 128), BF16)
+    far = lax.cond(longest > LONG, lambda v: exchange(v)[last], none, x)
+    return first, got, far
+
+
 def make_rhs(first, text_lanes):
     wide = pltpu.VMEM((OWN * 152, 128), F32)
     return call(
@@ -330,6 +385,7 @@
 
 
 def run_search(chunk, first_row, *operands):
+    more = (pltpu.VMEM((OWN // 4, ROWS, 128), BF16), pltpu.SemaphoreType.DMA) if chunk else ()
     return call(
         functools.partial(search, chunk, first_row),
         jax.ShapeDtypeStruct((OWN, 8, 128), F32),
@@ -339,8 +395,10 @@
             pltpu.VMEM((FR // 8, 8, NN), F32),
             pltpu.VMEM((FB, NN), F32),
             pltpu.VMEM((FB, NN), F32),
+            *more,
         ),
         smem=(0,),
+        hbm=(7,) if chunk else (),
     )(*operands)
 
 
@@ -375,25 +433,21 @@
     return jnp.concatenate([(longest + MB - 1) // MB, (longest + 2 * FB - 1) // (2 * FB)])
 
 
-def over_groups(x):
-    x = x + lax.ppermute(x, "dp_1", [(0, 1), (1, 0)])
-    for n in (1, 2):
-        x = x + lax.ppermute(x, "dp_0", [(i, (i + n) % 4) for i in range(4)])
-    return x
-
-
 def shards(means, log_scales, latents, text_lens, frame_lens):
     own = lax.axis_index(SEQ).astype(jnp.int32)
     rank = ranks(frame_lens)
     text_own, frame_own = owned(text_lens, rank, own), owned(frame_lens, rank, own)
     means, log_scales, latents = (jnp.transpose(x, (1, 2, 0)) for x in (means, log_scales, latents))
-    first = exchange(pack_call(pack_first, 2 * PROWS + ROWS, rank, means, log_scales, latents))
-    second = exchange(pack_call(pack_second, ROWS, rank, latents))
+    packed = pack_call(pack_first, 2 * PROWS + ROWS, rank, means, log_scales, latents)
+    packed, later_rank, latents, later_lens = lax.optimization_barrier((packed, rank, latents, frame_lens))
+    first = exchange(packed)
+    packed = pack_call(pack_second, ROWS, later_rank, latents)
+    first, second, far = exchange_short(first, packed, later_rank, later_lens)
     text_lanes, frame_lanes, counts = lanes_of(text_own), lanes_of(frame_own), counts_of(frame_own)
     rhs0, rhs1, bias0, bias1 = make_rhs(first, text_lanes)
     back = run_search(0, 2 * PROWS, counts, first, rhs0, bias0, text_lanes, frame_lanes)
-    back = exchange(run_search(1, 0, counts, second, rhs1, bias1, text_lanes, frame_lanes, back))
-    sums = over_groups(sum_up(back, frame_lens))
+    back = exchange(run_search(1, 0, counts, second, rhs1, bias1, text_lanes, frame_lanes, back, far))
+    sums = over_dp(sum_up(back, frame_lens), jnp.add)
     pos = call(
         unpack, jax.ShapeDtypeStruct((FB, GRP), F32), 2, (pltpu.VMEM((128, 2 * 128), F32),)
     )(rank, back.reshape(OWN * 8, 128))

time: 242 us -> 233 us (0.963)
  waiting for transfers between devices: 137 us -> 114 us
  starting transfers between devices: 31.4 us -> 41.1 us
  other arithmetic: 1.97 us -> 5.89 us
    all_to_all x3, waiting for transfers between devices: 131 us -> 67.7 us  [exchange(): return lax.all_to_all(x, SEQ, split_axis=0, concat_axis=0, tiled=True)]
    ppermute x3 -> x9, waiting for transfers between devices: 6.2 us -> 46.1 us  [the longest x3 31.3 us: exchange_short(): relayed = [lax.ppermute(x[:, CUT:], 'seq_0', [(i, 3)]) for i in range(3)]]
    ppermute x3 -> x9, starting transfers between devices: 4.82 us -> 13.7 us  [the longest x3 8.05 us: exchange_short(): relayed = [lax.ppermute(x[:, CUT:], 'seq_0', [(i, 3)]) for i in range(3)]]
    select_n x0 -> x1, other arithmetic: none -> 3.25 us  [exchange_short(): send = jnp.where(lax.axis_index('seq_0') == 3, relayed, x[:, :CUT])]
  transfers between devices with their start and end apart: 6 -> 12, of which waited for: 6 -> 10; matrix products, arithmetic and copies ran while one was open for 1% -> 2% of each run, Pallas kernels for 14% -> 14%
where the time goes in v4:
time: 233 us; the launch traced here: 232 us
  waiting for transfers between devices  114 us (49%)
  Pallas kernels  52.9 us (23%)
  starting transfers between devices  41.1 us (18%)
  local copies, waits for them, and re-layouts  13.8 us (6%)
  other arithmetic  5.89 us (3%)
  between operations  4.72 us (2%)
    all_to_all x3, waiting for transfers between devices, exchange(): return lax.all_to_all(x, SEQ, split_axis=0, concat_axis=0, tiled=True)  67.7 us
    pallas_call x2, Pallas kernels, run_search(): call(functools.partial(search, chunk, first_row), jax.ShapeDtypeStruct((O...  38.9 us
    ppermute x3, waiting for transfers between devices, exchange_short(): relayed = [lax.ppermute(x[:, CUT:], 'seq_0', [(i, 3)]) for i in range(3)]  31.3 us
    all_to_all x3, starting transfers between devices, exchange(): return lax.all_to_all(x, SEQ, split_axis=0, concat_axis=0, tiled=True)  27.4 us
    ppermute x4, waiting for transfers between devices, over_dp(): lax.ppermute(x, 'dp_0', [(i, (i + n) % 4) for i in range(4)])  12.9 us
    unnamed x20, local copies, waits for them, and re-layouts  12.5 us
    ppermute x3, starting transfers between devices, exchange_short(): relayed = [lax.ppermute(x[:, CUT:], 'seq_0', [(i, 3)]) for i in range(3)]  8.05 us
    pallas_call x2, Pallas kernels, pack_call(): call(body, jax.ShapeDtypeStruct((OWN, rows, 128), BF16), len(operands), (...  6.81 us
  transfers between devices with their start and end apart: 12, of which 10 were waited for; matrix products, arithmetic and copies ran while one was open for 2% of the time, Pallas kernels for 14%

profile of v4, /device:TPU:32, one launch (start us, length us, event | category | flops | bytes accessed | tf_op | source)
XLA Modules:
  0.0 232.1 jit_solution(10166575425139857203)
XLA Ops:
  1.5 2.3 %copy-done = bf16[256,48,192]{0,2,1:T(8,128)(2,1)S(1)} copy-done((bf16[256,48,192]{0,2,1:T(8,128)(2,1)S(1)}, bf16[256,48,192]{0,2,1:T(8,128)(2,1)}, u32[]{:S(2)}) %copy-start) | copy-done | bytes 4718616
  6.4 4.3 %shard_map.68 = bf16[32,576,128]{2,1,0:T(8,128)(2,1)S(1)} custom-call(s32[1,256]{1,0:T(1,128)S(1)} %bitcast.18, bf16[12,192,256]{2,1,0:T(8,128)(2,1)S(1)} %bitcast.15, bf16[12,192,256]{2,1,0:T(8,128)(2,1)S(1)} %bitcast.16, bf16[48,192,256]{2,1,0:T(8,128)(2,1)S(1)} %bitcast.13), custom_call_target="tpu_custom_call" | custom-call | tf_op jit(solution)/shard_map/pallas_call | solution.py:406
  10.7 2.2 copy-done.2
  12.9 11.2 %all-to-all-start.1 = ((bf16[32,576,128]{2,1,0:T(8,128)(2,1)}), bf16[32,576,128]{2,1,0:T(8,128)(2,1)}, u32[]{:S(2)}, u32[]{:S(2)}) async-start(bf16[32,576,128]{2,1,0:T(8,128)(2,1)} %copy-done.2), calls=%async_computation.1 | async-start | bytes 9437184 | tf_op jit(solution)/shard_map/all_to_all | solution.py:351
  24.1 2.3 %copy-done.1 = bf16[256,48,192]{0,2,1:T(8,128)(2,1)S(1)} copy-done((bf16[256,48,192]{0,2,1:T(8,128)(2,1)S(1)}, bf16[256,48,192]{0,2,1:T(8,128)(2,1)}, u32[]{:S(2)}) %copy-start.1) | copy-done | bytes 4718616
  26.4 2.5 %shard_map.69 = bf16[32,288,128]{2,1,0:T(8,128)(2,1)S(1)} custom-call(s32[1,256]{1,0:T(1,128)S(1)} %bitcast.19, bf16[48,192,256]{2,1,0:T(8,128)(2,1)S(1)} %bitcast.14), custom_call_target="tpu_custom_call" | custom-call | tf_op jit(solution)/shard_map/pallas_call | solution.py:406
  29.0 1.5 collective-permute-start.2
  30.5 1.4 collective-permute-start.1
  32.0 5.1 %collective-permute-start = (bf16[32,64,128]{2,1,0:T(8,128)(2,1)S(1)}, bf16[32,64,128]{2,1,0:T(8,128)(2,1)}, u32[]{:S(2)}, u32[]{:S(2)}) collective-permute-start(bf16[32,64,128]{2,1,0:T(8,128)(2,1)S(1)} %slice.30), channel_id=1, source_target_pairs={{0,24},{1,25},{2,26},{3,27},{4,28},{5,29},{6,30},{7,31},{32,56},{3... | collective-permute-start | bytes 1572872 | tf_op jit(solution)/shard_map/ppermute | solution.py:362
  37.1 31.3 %collective-permute-done = bf16[32,64,128]{2,1,0:T(8,128)(2,1)} collective-permute-done((bf16[32,64,128]{2,1,0:T(8,128)(2,1)S(1)}, bf16[32,64,128]{2,1,0:T(8,128)(2,1)}, u32[]{:S(2)}, u32[]{:S(2)}) %collective-permute-start) | collective-permute-done | bytes 524320 | tf_op jit(solution)/shard_map/ppermute | solution.py:362
  68.5 3.2 %slice_select_fusion = bf16[32,224,128]{2,1,0:T(8,128)(2,1)} fusion(bf16[32,288,128]{2,1,0:T(8,128)(2,1)S(1)} %shard_map.69, bf16[32,32,128]{2,1,0:T(8,128)(2,1)S(1)} %slice.31, bf16[32,64,128]{2,1,0:T(8,128)(2,1)} %collective-permute-done.2, bf16[32,64,128]{2,1,0:T(8,128)(2,1)} %collective-permute-done.1, bf16[32,64,128]{2,1,0:T(8,128)(2,1)} %collective-permute-done, ...), kind=kLoop, calls=%fused_computation | loop fusion | flops 8257536 | bytes 5505025 | tf_op jit(solution)/shard_map/jit(_where)/select_n | solution.py:364
  71.7 59.1 %all-to-all-done.1.y_ref = bf16[32,576,128]{2,1,0:T(8,128)(2,1)} async-done(((bf16[32,576,128]{2,1,0:T(8,128)(2,1)}), bf16[32,576,128]{2,1,0:T(8,128)(2,1)}, u32[]{:S(2)}, u32[]{:S(2)}) %all-to-all-start.1) | async-done | bytes 4718624 | tf_op jit(solution)/shard_map/all_to_all | solution.py:351
  130.8 8.5 %all-to-all-start.2 = ((bf16[32,224,128]{2,1,0:T(8,128)(2,1)}), bf16[32,224,128]{2,1,0:T(8,128)(2,1)S(1)}, u32[]{:S(2)}, u32[]{:S(2)}) async-start(bf16[32,224,128]{2,1,0:T(8,128)(2,1)} %slice_select_fusion), calls=%async_computation.2 | async-start | bytes 3670016 | tf_op jit(solution)/shard_map/all_to_all | solution.py:351
  143.3 3.4 %collective-permute-done.4 = f32[1,128]{1,0:T(1,128)S(1)} collective-permute-done((f32[1,128]{1,0:T(1,128)S(1)}, f32[1,128]{1,0:T(1,128)S(1)}, u32[]{:S(2)}, u32[]{:S(2)}) %collective-permute-start.4) | collective-permute-done | bytes 544 | tf_op jit(solution)/shard_map/ppermute | solution.py:357
  146.7 1.8 collective-permute-start.5
  148.9 2.8 %collective-permute-done.5 = f32[1,128]{1,0:T(1,128)S(1)} collective-permute-done((f32[1,128]{1,0:T(1,128)S(1)}, f32[1,128]{1,0:T(1,128)S(1)}, u32[]{:S(2)}, u32[]{:S(2)}) %collective-permute-start.5) | collective-permute-done | bytes 544 | tf_op jit(solution)/shard_map/ppermute | solution.py:357
  151.8 6.3 %shard_map.70 = (bf16[2,768,768]{2,1,0:T(8,128)(2,1)S(1)}, bf16[2,768,768]{2,1,0:T(8,128)(2,1)S(1)}, f32[8,1536]{1,0:T(8,128)S(1)}, f32[8,1536]{1,0:T(8,128)S(1)}) custom-call(bf16[32,576,128]{2,1,0:T(8,128)(2,1)} %all-to-all-done.1.y_ref, s32[2,8,128]{2,1,0:T(8,128)S(1)} %broadcast_in_dim.68.text_ref), custom_call_target="tpu_custom_call" | custom-call | tf_op jit(solution)/shard_map/pallas_call | solution.py:378
  159.5 23.7 %shard_map.71.rest_0_ = f32[32,8,128]{2,1,0:T(8,128)S(1)} custom-call(s32[4]{0:T(128)S(1)} %pad_add_fusion.count_ref, bf16[32,576,128]{2,1,0:T(8,128)(2,1)} %all-to-all-done.1.y_ref, bf16[2,768,768]{2,1,0:T(8,128)(2,1)S(1)} %get-tuple-element.27.rhs_ref, f32[8,1536]{1,0:T(8,128)S(1)} %get-tuple-element.28.bias_ref, ...), custom_call_target="tpu_custom_call" | custom-call | tf_op jit(solution)/shard_map/pallas_call | solution.py:389
  183.4 1.7 copy-done.4
  185.1 15.2 %shard_map.72 = f32[32,8,128]{2,1,0:T(8,128)} custom-call(s32[4]{0:T(128)S(1)} %pad_add_fusion.count_ref, bf16[32,224,128]{2,1,0:T(8,128)(2,1)S(1)} %all-to-all-done.2.y_ref, bf16[2,768,768]{2,1,0:T(8,128)(2,1)S(1)} %copy-done.4, f32[8,1536]{1,0:T(8,128)S(1)} %get-tuple-element.26.bias_ref, s32[2,8,128]{2,1,0:T(8,128)S(1)} %broadcast_in_dim.68.text_ref, ...), custom_call_target="tpu_custom_call" | custom-call | tf_op jit(solution)/shard_map/pallas_call | solution.py:389
  200.3 7.7 %all-to-all-start.3 = ((f32[32,8,128]{2,1,0:T(8,128)}), f32[32,8,128]{2,1,0:T(8,128)S(1)}, u32[]{:S(2)}, u32[]{:S(2)}) async-start(f32[32,8,128]{2,1,0:T(8,128)} %shard_map.72), calls=%async_computation.3 | async-start | bytes 262144 | tf_op jit(solution)/shard_map/all_to_all | solution.py:351
  209.3 8.4 %all-to-all-done.3 = f32[32,8,128]{2,1,0:T(8,128)S(1)} async-done(((f32[32,8,128]{2,1,0:T(8,128)}), f32[32,8,128]{2,1,0:T(8,128)S(1)}, u32[]{:S(2)}, u32[]{:S(2)}) %all-to-all-start.3) | async-done | bytes 131104 | tf_op jit(solution)/shard_map/all_to_all | solution.py:351
  220.2 3.7 %collective-permute-done.7 = f32[1,128]{1,0:T(1,128)S(1)} collective-permute-done((f32[1,128]{1,0:T(1,128)S(1)}, f32[1,128]{1,0:T(1,128)S(1)}, u32[]{:S(2)}, u32[]{:S(2)}) %collective-permute-start.7) | collective-permute-done | bytes 544 | tf_op jit(solution)/shard_map/ppermute | solution.py:357
  225.9 3.0 %collective-permute-done.8 = f32[1,128]{1,0:T(1,128)S(1)} collective-permute-done((f32[1,128]{1,0:T(1,128)S(1)}, f32[1,128]{1,0:T(1,128)S(1)}, u32[]{:S(2)}, u32[]{:S(2)}) %collective-permute-start.8) | collective-permute-done | bytes 544 | tf_op jit(solution)/shard_map/ppermute | solution.py:357
  (58 shorter events, 14.8 us)
Async XLA Ops:
  1.5 2.3 %copy-start = (bf16[256,48,192]{0,2,1:T(8,128)(2,1)S(1)}, bf16[256,48,192]{0,2,1:T(8,128)(2,1)}, u32[]{:S(2)}) copy-start(bf16[256,48,192]{0,2,1:T(8,128)(2,1)} %param.9) | copy-start | bytes 14155780
  3.9 1.3 copy-start.5
  5.1 1.3 copy-start.6
  10.7 2.2 copy-start.2
  12.9 118.0 %all-to-all-start.1 = ((bf16[32,576,128]{2,1,0:T(8,128)(2,1)}), bf16[32,576,128]{2,1,0:T(8,128)(2,1)}, u32[]{:S(2)}, u32[]{:S(2)}) async-start(bf16[32,576,128]{2,1,0:T(8,128)(2,1)} %copy-done.2), calls=%async_computation.1 | async-start | bytes 9437184 | tf_op jit(solution)/shard_map/all_to_all | solution.py:351
  24.1 2.3 %copy-start.1 = (bf16[256,48,192]{0,2,1:T(8,128)(2,1)S(1)}, bf16[256,48,192]{0,2,1:T(8,128)(2,1)}, u32[]{:S(2)}) copy-start(bf16[256,48,192]{0,2,1:T(8,128)(2,1)} %param.9) | copy-start | bytes 14155780
  29.0 101.9 %copy-start.7 = (bf16[32,288,128]{2,1,0:T(8,128)(2,1)}, bf16[32,288,128]{2,1,0:T(8,128)(2,1)S(1)}, u32[]{:S(2)}) copy-start(bf16[32,288,128]{2,1,0:T(8,128)(2,1)S(1)} %shard_map.69) | copy-start | bytes 7077892
  29.0 8.1 %collective-permute-start.2 = (bf16[32,64,128]{2,1,0:T(8,128)(2,1)S(1)}, bf16[32,64,128]{2,1,0:T(8,128)(2,1)}, u32[]{:S(2)}, u32[]{:S(2)}) collective-permute-start(bf16[32,64,128]{2,1,0:T(8,128)(2,1)S(1)} %slice.30), channel_id=1, source_target_pairs={{16,24},{17,25},{18,26},{19,27},{20,28},{21,29},{22,30},{23,31},{4... | collective-permute-start | bytes 1572872 | tf_op jit(solution)/shard_map/ppermute | solution.py:362
  30.5 6.6 %collective-permute-start.1 = (bf16[32,64,128]{2,1,0:T(8,128)(2,1)S(1)}, bf16[32,64,128]{2,1,0:T(8,128)(2,1)}, u32[]{:S(2)}, u32[]{:S(2)}) collective-permute-start(bf16[32,64,128]{2,1,0:T(8,128)(2,1)S(1)} %slice.30), channel_id=1, source_target_pairs={{8,24},{9,25},{10,26},{11,27},{12,28},{13,29},{14,30},{15,31},{40,... | collective-permute-start | bytes 1572872 | tf_op jit(solution)/shard_map/ppermute | solution.py:362
  32.0 36.5 %collective-permute-start = (bf16[32,64,128]{2,1,0:T(8,128)(2,1)S(1)}, bf16[32,64,128]{2,1,0:T(8,128)(2,1)}, u32[]{:S(2)}, u32[]{:S(2)}) collective-permute-start(bf16[32,64,128]{2,1,0:T(8,128)(2,1)S(1)} %slice.30), channel_id=1, source_target_pairs={{0,24},{1,25},{2,26},{3,27},{4,28},{5,29},{6,30},{7,31},{32,56},{3... | collective-permute-start | bytes 1572872 | tf_op jit(solution)/shard_map/ppermute | solution.py:362
  71.7 67.6 %copy-start.8 = (s32[256]{0:T(256)S(1)}, s32[256]{0:T(256)}, u32[]{:S(2)}) copy-start(s32[256]{0:T(256)} %param.11) | copy-start | bytes 3076
  71.7 69.1 %copy-start.9 = (s32[256]{0:T(256)S(1)}, s32[256]{0:T(256)}, u32[]{:S(2)}) copy-start(s32[256]{0:T(256)} %param.10) | copy-start | bytes 3076
  130.8 52.4 %all-to-all-start.2 = ((bf16[32,224,128]{2,1,0:T(8,128)(2,1)}), bf16[32,224,128]{2,1,0:T(8,128)(2,1)S(1)}, u32[]{:S(2)}, u32[]{:S(2)}) async-start(bf16[32,224,128]{2,1,0:T(8,128)(2,1)} %slice_select_fusion), calls=%async_computation.2 | async-start | bytes 3670016 | tf_op jit(solution)/shard_map/all_to_all | solution.py:351
  140.6 1.2 collective-permute-start.3
  141.9 4.8 %collective-permute-start.4 = (f32[1,128]{1,0:T(1,128)S(1)}, f32[1,128]{1,0:T(1,128)S(1)}, u32[]{:S(2)}, u32[]{:S(2)}) collective-permute-start(f32[1,128]{1,0:T(1,128)S(1)} %broadcast_maximum_fusion), channel_id=1, source_target_pairs={{0,64},{64,128},{128,192},{192,0},{1,65},{65,129},{129,193},{193,1... | collective-permute-start | bytes 1544 | tf_op jit(solution)/shard_map/ppermute | solution.py:357
  146.7 5.1 %collective-permute-start.5 = (f32[1,128]{1,0:T(1,128)S(1)}, f32[1,128]{1,0:T(1,128)S(1)}, u32[]{:S(2)}, u32[]{:S(2)}) collective-permute-start(f32[1,128]{1,0:T(1,128)S(1)} %fusion.6), channel_id=1, source_target_pairs={{0,128},{64,192},{128,0},{192,64},{1,129},{65,193},{129,1},{193,65... | collective-permute-start | bytes 1544 | tf_op jit(solution)/shard_map/ppermute | solution.py:357
  158.0 1.4 copy-start.3
  183.4 1.7 copy-start.4
  200.3 17.4 %all-to-all-start.3 = ((f32[32,8,128]{2,1,0:T(8,128)}), f32[32,8,128]{2,1,0:T(8,128)S(1)}, u32[]{:S(2)}, u32[]{:S(2)}) async-start(f32[32,8,128]{2,1,0:T(8,128)} %shard_map.72), calls=%async_computation.3 | async-start | bytes 262144 | tf_op jit(solution)/shard_map/all_to_all | solution.py:351
  217.8 1.2 collective-permute-start.6
  219.0 4.8 %collective-permute-start.7 = (f32[1,128]{1,0:T(1,128)S(1)}, f32[1,128]{1,0:T(1,128)S(1)}, u32[]{:S(2)}, u32[]{:S(2)}) collective-permute-start(f32[1,128]{1,0:T(1,128)S(1)} %fusion.5), channel_id=1, source_target_pairs={{0,64},{64,128},{128,192},{192,0},{1,65},{65,129},{129,193},{193,1... | collective-permute-start | bytes 1544 | tf_op jit(solution)/shard_map/ppermute | solution.py:357
  223.8 5.1 %collective-permute-start.8 = (f32[1,128]{1,0:T(1,128)S(1)}, f32[1,128]{1,0:T(1,128)S(1)}, u32[]{:S(2)}, u32[]{:S(2)}) collective-permute-start(f32[1,128]{1,0:T(1,128)S(1)} %add.38), channel_id=1, source_target_pairs={{0,128},{64,192},{128,0},{192,64},{1,129},{65,193},{129,1},{193,65... | collective-permute-start | bytes 1544 | tf_op jit(solution)/shard_map/ppermute | solution.py:357

commit v5 on v4

--- a/solution.py
+++ b/solution.py
@@ -85,10 +85,12 @@
     lax.fori_loop(0, TB // TOKEN_UNROLL, tokens, 0)
 
 
-def stage_latents(chunk, rank_ref, lat_ref, stage):
+def stage_latents(chunk, rank_ref, lat_ref, stage, ready=None):
     picks = one_hot(rank_ref[...], chunk * NU * OWN, NU * OWN, BF16)
 
     def frames(j, _):
+        if ready:
+            ready(j)
         for q in range(FRAME_UNROLL):
             frame = j * FRAME_UNROLL + q
             pack_block(lat_ref[frame], picks, stage, frame, frame + NU * FB, FB, NU)
@@ -102,11 +104,50 @@
         out_ref[d, first : first + rows, :] = stage[d * PAD : d * PAD + rows, :].astype(BF16)
 
 
-def pack_first(rank_ref, means_ref, logs_ref, lat_ref, out_ref, stage):
-    stage_priors(rank_ref, means_ref, logs_ref, stage)
-    unstage(stage, out_ref, 0, 2 * PROWS)
-    stage_latents(0, rank_ref, lat_ref, stage)
-    unstage(stage, out_ref, 2 * PROWS, ROWS)
+def pack_first(rank_ref, means_hbm, logs_hbm, lat_hbm, out_hbm, stage, means, logs, lat, out0, out1, sems):
+    def piece(j):
+        part = pl.ds(j * FRAME_UNROLL, FRAME_UNROLL)
+        return pltpu.make_async_copy(lat_hbm.at[part], lat.at[part], sems.at[4 + j])
+
+    priors = [
+        pltpu.make_async_copy(means_hbm, means, sems.at[0]),
+        pltpu.make_async_copy(logs_hbm, logs, sems.at[1]),
+    ]
+    outs = [
+        pltpu.make_async_copy(out0, out_hbm.at[:, pl.ds(0, 2 * PROWS)], sems.at[2]),
+        pltpu.make_async_copy(out1, out_hbm.at[:, pl.ds(2 * PROWS, ROWS)], sems.at[3]),
+    ]
+    for copy in (*priors, *(piece(j) for j in range(FB // FRAME_UNROLL))):
+        copy.start()
+    for copy in priors:
+        copy.wait()
+    stage_priors(rank_ref, means, logs, stage)
+    unstage(stage, out0, 0, 2 * PROWS)
+    outs[0].start()
+    stage_latents(0, rank_ref, lat, stage, lambda j: piece(j).wait())
+    unstage(stage, out1, 0, ROWS)
+    outs[1].start()
+    for copy in outs:
+        copy.wait()
+
+
+def pack_whole(rank, means, log_scales, latents):
+    hbm, vmem = pl.BlockSpec(memory_space=pltpu.HBM), pl.BlockSpec(memory_space=pltpu.VMEM)
+    half = pltpu.VMEM((OWN, ROWS, 128), BF16)
+    return pl.pallas_call(
+        pack_first,
+        out_shape=jax.ShapeDtypeStruct((OWN, 2 * PROWS + ROWS, 128), BF16),
+        in_specs=[vmem, hbm, hbm, hbm],
+        out_specs=hbm,
+        scratch_shapes=[
+            pltpu.VMEM((OWN * PAD, 128), F32),
+            *(pltpu.VMEM(x.shape, BF16) for x in (means, log_scales, latents)),
+            half,
+            half,
+            pltpu.SemaphoreType.DMA((4 + FB // FRAME_UNROLL,)),
+        ],
+        compiler_params=pltpu.CompilerParams(vmem_limit_bytes=63 * 1024 * 1024),
+    )(rank, means, log_scales, latents)
 
 
 def pack_second(rank_ref, lat_ref, out_ref, stage):
@@ -362,10 +403,10 @@
     relayed = [lax.ppermute(x[:, CUT:], "seq_0", [(i, 3)]) for i in range(3)]
     relayed = jnp.concatenate([*relayed, x[:, : CUT - 3 * (ROWS - CUT)]], axis=1)
     send = jnp.where(lax.axis_index("seq_0") == 3, relayed, x[:, :CUT])
-    first, send = lax.optimization_barrier((first, send))
-    got = exchange(send)
     longest = jnp.max(jnp.where(rank[0] >= NU * OWN, frame_lens, 0)).astype(F32)
     longest = over_dp(jnp.full((1, 128), longest), jnp.maximum)[0, 0]
+    first, send, longest = lax.optimization_barrier((first, send, longest))
+    got = exchange(send)
     last = slice(3 * OWN // 4, OWN)
     got, longest = lax.optimization_barrier((got, longest))
     none = lambda v: jnp.zeros((OWN // 4, ROWS, 128), BF16)
@@ -438,7 +479,7 @@
     rank = ranks(frame_lens)
     text_own, frame_own = owned(text_lens, rank, own), owned(frame_lens, rank, own)
     means, log_scales, latents = (jnp.transpose(x, (1, 2, 0)) for x in (means, log_scales, latents))
-    packed = pack_call(pack_first, 2 * PROWS + ROWS, rank, means, log_scales, latents)
+    packed = pack_whole(rank, means, log_scales, latents)
     packed, later_rank, latents, later_lens = lax.optimization_barrier((packed, rank, latents, frame_lens))
     first = exchange(packed)
     packed = pack_call(pack_second, ROWS, later_rank, latents)

time: 233 us -> 229 us (0.983)
  local copies, waits for them, and re-layouts: 13.8 us -> 6.7 us
  Pallas kernels: 52.9 us -> 57.6 us
    ppermute x3, waiting for transfers between devices: 31.3 us -> 18.9 us  [exchange_short(): relayed = [lax.ppermute(x[:, CUT:], 'seq_0', [(i, 3)]) for i in range(3)]]
    all_to_all x3, waiting for transfers between devices: 67.7 us -> 78.9 us  [exchange(): return lax.all_to_all(x, SEQ, split_axis=0, concat_axis=0, tiled=True)]
    pallas_call x0 -> x1, Pallas kernels: none -> 8.09 us  [pack_whole(): pl.pallas_call(pack_first, out_shape=jax.ShapeDtypeStruct((OWN, 2 * PROWS...]
    unnamed x20 -> x14, local copies, waits for them, and re-layouts: 12.5 us -> 5.45 us
    pallas_call x2 -> x1, Pallas kernels: 6.81 us -> 2.52 us  [pack_call(): call(body, jax.ShapeDtypeStruct((OWN, rows, 128), BF16), len(operands), (...]
  transfers between devices with their start and end apart: 12 -> 12, of which waited for: 10 -> 10; matrix products, arithmetic and copies ran while one was open for 2% -> 2% of each run, Pallas kernels for 14% -> 15%
where the time goes in v5:
time: 229 us; the launch traced here: 228 us
  waiting for transfers between devices  112 us (49%)
  Pallas kernels  57.6 us (25%)
  starting transfers between devices  40.9 us (18%)
  local copies, waits for them, and re-layouts  6.7 us (3%)
  other arithmetic  6.46 us (3%)
  between operations  4.62 us (2%)
    all_to_all x3, waiting for transfers between devices, exchange(): return lax.all_to_all(x, SEQ, split_axis=0, concat_axis=0, tiled=True)  78.9 us
    pallas_call x2, Pallas kernels, run_search(): call(functools.partial(search, chunk, first_row), jax.ShapeDtypeStruct((O...  39.9 us
    all_to_all x3, starting transfers between devices, exchange(): return lax.all_to_all(x, SEQ, split_axis=0, concat_axis=0, tiled=True)  25.4 us
    ppermute x3, waiting for transfers between devices, exchange_short(): relayed = [lax.ppermute(x[:, CUT:], 'seq_0', [(i, 3)]) for i in range(3)]  18.9 us
    ppermute x4, waiting for transfers between devices, over_dp(): lax.ppermute(x, 'dp_0', [(i, (i + n) % 4) for i in range(4)])  11.5 us
    pallas_call x1, Pallas kernels, pack_whole(): pl.pallas_call(pack_first, out_shape=jax.ShapeDtypeStruct((OWN, 2 * PROWS...  8.09 us
    ppermute x3, starting transfers between devices, exchange_short(): relayed = [lax.ppermute(x[:, CUT:], 'seq_0', [(i, 3)]) for i in range(3)]  8.07 us
    ppermute x4, starting transfers between devices, over_dp(): lax.ppermute(x, 'dp_0', [(i, (i + n) % 4) for i in range(4)])  7.25 us
  transfers between devices with their start and end apart: 12, of which 10 were waited for; matrix products, arithmetic and copies ran while one was open for 2% of the time, Pallas kernels for 15%

profile of v5, /device:TPU:32, one launch (start us, length us, event | category | flops | bytes accessed | tf_op | source)
XLA Modules:
  0.0 227.9 jit_solution(10299947036013270219)
XLA Ops:
  2.1 8.1 %shard_map.68 = bf16[32,576,128]{2,1,0:T(8,128)(2,1)} custom-call(s32[1,256]{1,0:T(1,128)} %bitcast.16, bf16[12,192,256]{2,1,0:T(8,128)(2,1)} %bitcast.20, bf16[12,192,256]{2,1,0:T(8,128)(2,1)} %bitcast.21, bf16[48,192,256]{2,1,0:T(8,128)(2,1)} %bitcast.13), custom_call_target="tpu_custom_call" | custom-call | tf_op jit(solution)/shard_map/pallas_call | solution.py:137
  10.2 11.2 %all-to-all-start.1 = ((bf16[32,576,128]{2,1,0:T(8,128)(2,1)}), bf16[32,576,128]{2,1,0:T(8,128)(2,1)}, u32[]{:S(2)}, u32[]{:S(2)}) async-start(bf16[32,576,128]{2,1,0:T(8,128)(2,1)} %shard_map.68), calls=%async_computation.1 | async-start | bytes 9437184 | tf_op jit(solution)/shard_map/all_to_all | solution.py:392
  21.4 2.3 %copy-done = bf16[256,48,192]{0,2,1:T(8,128)(2,1)S(1)} copy-done((bf16[256,48,192]{0,2,1:T(8,128)(2,1)S(1)}, bf16[256,48,192]{0,2,1:T(8,128)(2,1)}, u32[]{:S(2)}) %copy-start) | copy-done | bytes 4718616
  23.8 2.5 %shard_map.69 = bf16[32,288,128]{2,1,0:T(8,128)(2,1)S(1)} custom-call(s32[1,256]{1,0:T(1,128)S(1)} %bitcast.17, bf16[48,192,256]{2,1,0:T(8,128)(2,1)S(1)} %bitcast.14), custom_call_target="tpu_custom_call" | custom-call | tf_op jit(solution)/shard_map/pallas_call | solution.py:447
  29.3 5.1 %collective-permute-start = (bf16[32,64,128]{2,1,0:T(8,128)(2,1)S(1)}, bf16[32,64,128]{2,1,0:T(8,128)(2,1)}, u32[]{:S(2)}, u32[]{:S(2)}) collective-permute-start(bf16[32,64,128]{2,1,0:T(8,128)(2,1)S(1)} %slice.30), channel_id=1, source_target_pairs={{0,24},{1,25},{2,26},{3,27},{4,28},{5,29},{6,30},{7,31},{32,56},{3... | collective-permute-start | bytes 1572872 | tf_op jit(solution)/shard_map/ppermute | solution.py:403
  37.0 1.6 collective-permute-start.4
  38.6 3.2 %collective-permute-done.4 = f32[1,128]{1,0:T(1,128)S(1)} collective-permute-done((f32[1,128]{1,0:T(1,128)S(1)}, f32[1,128]{1,0:T(1,128)S(1)}, u32[]{:S(2)}, u32[]{:S(2)}) %collective-permute-start.4) | collective-permute-done | bytes 544 | tf_op jit(solution)/shard_map/ppermute | solution.py:398
  41.8 2.0 collective-permute-start.5
  43.8 3.1 %collective-permute-done.5 = f32[1,128]{1,0:T(1,128)S(1)} collective-permute-done((f32[1,128]{1,0:T(1,128)S(1)}, f32[1,128]{1,0:T(1,128)S(1)}, u32[]{:S(2)}, u32[]{:S(2)}) %collective-permute-start.5) | collective-permute-done | bytes 544 | tf_op jit(solution)/shard_map/ppermute | solution.py:398
  46.9 18.9 %collective-permute-done = bf16[32,64,128]{2,1,0:T(8,128)(2,1)} collective-permute-done((bf16[32,64,128]{2,1,0:T(8,128)(2,1)S(1)}, bf16[32,64,128]{2,1,0:T(8,128)(2,1)}, u32[]{:S(2)}, u32[]{:S(2)}) %collective-permute-start) | collective-permute-done | bytes 524320 | tf_op jit(solution)/shard_map/ppermute | solution.py:403
  65.8 3.3 %slice_select_fusion = bf16[32,224,128]{2,1,0:T(8,128)(2,1)} fusion(bf16[32,288,128]{2,1,0:T(8,128)(2,1)S(1)} %shard_map.69, bf16[32,32,128]{2,1,0:T(8,128)(2,1)S(1)} %slice.31, bf16[32,64,128]{2,1,0:T(8,128)(2,1)} %collective-permute-done.2, bf16[32,64,128]{2,1,0:T(8,128)(2,1)} %collective-permute-done.1, bf16[32,64,128]{2,1,0:T(8,128)(2,1)} %collective-permute-done, ...), kind=kLoop, calls=%fused_computation | loop fusion | flops 8257536 | bytes 5505025 | tf_op jit(solution)/shard_map/jit(_where)/select_n | solution.py:405
  69.1 58.9 %all-to-all-done.1.y_ref = bf16[32,576,128]{2,1,0:T(8,128)(2,1)} async-done(((bf16[32,576,128]{2,1,0:T(8,128)(2,1)}), bf16[32,576,128]{2,1,0:T(8,128)(2,1)}, u32[]{:S(2)}, u32[]{:S(2)}) %all-to-all-start.1) | async-done | bytes 4718624 | tf_op jit(solution)/shard_map/all_to_all | solution.py:392
  127.9 8.5 %all-to-all-start.2 = ((bf16[32,224,128]{2,1,0:T(8,128)(2,1)}), bf16[32,224,128]{2,1,0:T(8,128)(2,1)S(1)}, u32[]{:S(2)}, u32[]{:S(2)}) async-start(bf16[32,224,128]{2,1,0:T(8,128)(2,1)} %slice_select_fusion), calls=%async_computation.2 | async-start | bytes 3670016 | tf_op jit(solution)/shard_map/all_to_all | solution.py:392
  137.4 6.3 %shard_map.70 = (bf16[2,768,768]{2,1,0:T(8,128)(2,1)S(1)}, bf16[2,768,768]{2,1,0:T(8,128)(2,1)S(1)}, f32[8,1536]{1,0:T(8,128)S(1)}, f32[8,1536]{1,0:T(8,128)S(1)}) custom-call(bf16[32,576,128]{2,1,0:T(8,128)(2,1)} %all-to-all-done.1.y_ref, s32[2,8,128]{2,1,0:T(8,128)S(1)} %broadcast_in_dim.68.text_ref), custom_call_target="tpu_custom_call" | custom-call | tf_op jit(solution)/shard_map/pallas_call | solution.py:419
  145.1 23.7 %shard_map.71.rest_0_ = f32[32,8,128]{2,1,0:T(8,128)S(1)} custom-call(s32[4]{0:T(128)S(1)} %pad_add_fusion.count_ref, bf16[32,576,128]{2,1,0:T(8,128)(2,1)} %all-to-all-done.1.y_ref, bf16[2,768,768]{2,1,0:T(8,128)(2,1)S(1)} %get-tuple-element.29.rhs_ref, f32[8,1536]{1,0:T(8,128)S(1)} %get-tuple-element.30.bias_ref, ...), custom_call_target="tpu_custom_call" | custom-call | tf_op jit(solution)/shard_map/pallas_call | solution.py:430
  168.8 11.7 %all-to-all-done.2.y_ref = bf16[32,224,128]{2,1,0:T(8,128)(2,1)S(1)} async-done(((bf16[32,224,128]{2,1,0:T(8,128)(2,1)}), bf16[32,224,128]{2,1,0:T(8,128)(2,1)S(1)}, u32[]{:S(2)}, u32[]{:S(2)}) %all-to-all-start.2) | async-done | bytes 1835040 | tf_op jit(solution)/shard_map/all_to_all | solution.py:392
  180.6 1.7 copy-done.2
  182.2 16.2 %shard_map.72 = f32[32,8,128]{2,1,0:T(8,128)} custom-call(s32[4]{0:T(128)S(1)} %pad_add_fusion.count_ref, bf16[32,224,128]{2,1,0:T(8,128)(2,1)S(1)} %all-to-all-done.2.y_ref, bf16[2,768,768]{2,1,0:T(8,128)(2,1)S(1)} %copy-done.2, f32[8,1536]{1,0:T(8,128)S(1)} %get-tuple-element.28.bias_ref, s32[2,8,128]{2,1,0:T(8,128)S(1)} %broadcast_in_dim.68.text_ref, ...), custom_call_target="tpu_custom_call" | custom-call | tf_op jit(solution)/shard_map/pallas_call | solution.py:430
  198.4 5.6 %all-to-all-start.3 = ((f32[32,8,128]{2,1,0:T(8,128)}), f32[32,8,128]{2,1,0:T(8,128)S(1)}, u32[]{:S(2)}, u32[]{:S(2)}) async-start(f32[32,8,128]{2,1,0:T(8,128)} %shard_map.72), calls=%async_computation.3 | async-start | bytes 262144 | tf_op jit(solution)/shard_map/all_to_all | solution.py:392
  205.3 8.4 %all-to-all-done.3 = f32[32,8,128]{2,1,0:T(8,128)S(1)} async-done(((f32[32,8,128]{2,1,0:T(8,128)}), f32[32,8,128]{2,1,0:T(8,128)S(1)}, u32[]{:S(2)}, u32[]{:S(2)}) %all-to-all-start.3) | async-done | bytes 131104 | tf_op jit(solution)/shard_map/all_to_all | solution.py:392
  215.0 1.7 collective-permute-start.7
  216.7 3.1 %collective-permute-done.7 = f32[1,128]{1,0:T(1,128)S(1)} collective-permute-done((f32[1,128]{1,0:T(1,128)S(1)}, f32[1,128]{1,0:T(1,128)S(1)}, u32[]{:S(2)}, u32[]{:S(2)}) %collective-permute-start.7) | collective-permute-done | bytes 544 | tf_op jit(solution)/shard_map/ppermute | solution.py:398
  219.8 2.0 collective-permute-start.8
  222.8 2.1 collective-permute-done.8
  (52 shorter events, 12.3 us)
Async XLA Ops:
  10.2 11.3 %copy-start.3 = (s32[256]{0:T(256)S(1)}, s32[256]{0:T(256)}, u32[]{:S(2)}) copy-start(s32[256]{0:T(256)} %convert_reduce_fusion) | copy-start | bytes 3076
  10.2 117.8 %all-to-all-start.1 = ((bf16[32,576,128]{2,1,0:T(8,128)(2,1)}), bf16[32,576,128]{2,1,0:T(8,128)(2,1)}, u32[]{:S(2)}, u32[]{:S(2)}) async-start(bf16[32,576,128]{2,1,0:T(8,128)(2,1)} %shard_map.68), calls=%async_computation.1 | async-start | bytes 9437184 | tf_op jit(solution)/shard_map/all_to_all | solution.py:392
  21.4 2.3 %copy-start = (bf16[256,48,192]{0,2,1:T(8,128)(2,1)S(1)}, bf16[256,48,192]{0,2,1:T(8,128)(2,1)}, u32[]{:S(2)}) copy-start(bf16[256,48,192]{0,2,1:T(8,128)(2,1)} %param.9) | copy-start | bytes 14155780
  23.8 10.7 %copy-start.5 = (s32[256]{0:T(256)S(1)}, s32[256]{0:T(256)}, u32[]{:S(2)}) copy-start(s32[256]{0:T(256)} %param.11) | copy-start | bytes 3076
  26.3 101.6 %copy-start.4 = (bf16[32,288,128]{2,1,0:T(8,128)(2,1)}, bf16[32,288,128]{2,1,0:T(8,128)(2,1)S(1)}, u32[]{:S(2)}) copy-start(bf16[32,288,128]{2,1,0:T(8,128)(2,1)S(1)} %shard_map.69) | copy-start | bytes 7077892
  26.4 20.5 %collective-permute-start.2 = (bf16[32,64,128]{2,1,0:T(8,128)(2,1)S(1)}, bf16[32,64,128]{2,1,0:T(8,128)(2,1)}, u32[]{:S(2)}, u32[]{:S(2)}) collective-permute-start(bf16[32,64,128]{2,1,0:T(8,128)(2,1)S(1)} %slice.30), channel_id=1, source_target_pairs={{16,24},{17,25},{18,26},{19,27},{20,28},{21,29},{22,30},{23,31},{4... | collective-permute-start | bytes 1572872 | tf_op jit(solution)/shard_map/ppermute | solution.py:403
  27.9 19.0 %collective-permute-start.1 = (bf16[32,64,128]{2,1,0:T(8,128)(2,1)S(1)}, bf16[32,64,128]{2,1,0:T(8,128)(2,1)}, u32[]{:S(2)}, u32[]{:S(2)}) collective-permute-start(bf16[32,64,128]{2,1,0:T(8,128)(2,1)S(1)} %slice.30), channel_id=1, source_target_pairs={{8,24},{9,25},{10,26},{11,27},{12,28},{13,29},{14,30},{15,31},{40,... | collective-permute-start | bytes 1572872 | tf_op jit(solution)/shard_map/ppermute | solution.py:403
  29.3 36.5 %collective-permute-start = (bf16[32,64,128]{2,1,0:T(8,128)(2,1)S(1)}, bf16[32,64,128]{2,1,0:T(8,128)(2,1)}, u32[]{:S(2)}, u32[]{:S(2)}) collective-permute-start(bf16[32,64,128]{2,1,0:T(8,128)(2,1)S(1)} %slice.30), channel_id=1, source_target_pairs={{0,24},{1,25},{2,26},{3,27},{4,28},{5,29},{6,30},{7,31},{32,56},{3... | collective-permute-start | bytes 1572872 | tf_op jit(solution)/shard_map/ppermute | solution.py:403
  35.8 1.2 collective-permute-start.3
  37.0 4.8 %collective-permute-start.4 = (f32[1,128]{1,0:T(1,128)S(1)}, f32[1,128]{1,0:T(1,128)S(1)}, u32[]{:S(2)}, u32[]{:S(2)}) collective-permute-start(f32[1,128]{1,0:T(1,128)S(1)} %broadcast_maximum_fusion), channel_id=1, source_target_pairs={{0,64},{64,128},{128,192},{192,0},{1,65},{65,129},{129,193},{193,1... | collective-permute-start | bytes 1544 | tf_op jit(solution)/shard_map/ppermute | solution.py:398
  41.8 5.1 %collective-permute-start.5 = (f32[1,128]{1,0:T(1,128)S(1)}, f32[1,128]{1,0:T(1,128)S(1)}, u32[]{:S(2)}, u32[]{:S(2)}) collective-permute-start(f32[1,128]{1,0:T(1,128)S(1)} %fusion.6), channel_id=1, source_target_pairs={{0,128},{64,192},{128,0},{192,64},{1,129},{65,193},{129,1},{193,65... | collective-permute-start | bytes 1544 | tf_op jit(solution)/shard_map/ppermute | solution.py:398
  69.1 67.4 %copy-start.6 = (s32[256]{0:T(256)S(1)}, s32[256]{0:T(256)}, u32[]{:S(2)}) copy-start(s32[256]{0:T(256)} %param.10) | copy-start | bytes 3076
  127.9 52.5 %all-to-all-start.2 = ((bf16[32,224,128]{2,1,0:T(8,128)(2,1)}), bf16[32,224,128]{2,1,0:T(8,128)(2,1)S(1)}, u32[]{:S(2)}, u32[]{:S(2)}) async-start(bf16[32,224,128]{2,1,0:T(8,128)(2,1)} %slice_select_fusion), calls=%async_computation.2 | async-start | bytes 3670016 | tf_op jit(solution)/shard_map/all_to_all | solution.py:392
  143.6 1.4 copy-start.1
  180.6 1.7 copy-start.2
  198.4 15.3 %all-to-all-start.3 = ((f32[32,8,128]{2,1,0:T(8,128)}), f32[32,8,128]{2,1,0:T(8,128)S(1)}, u32[]{:S(2)}, u32[]{:S(2)}) async-start(f32[32,8,128]{2,1,0:T(8,128)} %shard_map.72), calls=%async_computation.3 | async-start | bytes 262144 | tf_op jit(solution)/shard_map/all_to_all | solution.py:392
  213.8 1.2 collective-permute-start.6
  215.0 4.8 %collective-permute-start.7 = (f32[1,128]{1,0:T(1,128)S(1)}, f32[1,128]{1,0:T(1,128)S(1)}, u32[]{:S(2)}, u32[]{:S(2)}) collective-permute-start(f32[1,128]{1,0:T(1,128)S(1)} %fusion.5), channel_id=1, source_target_pairs={{0,64},{64,128},{128,192},{192,0},{1,65},{65,129},{129,193},{193,1... | collective-permute-start | bytes 1544 | tf_op jit(solution)/shard_map/ppermute | solution.py:398
  219.8 5.1 %collective-permute-start.8 = (f32[1,128]{1,0:T(1,128)S(1)}, f32[1,128]{1,0:T(1,128)S(1)}, u32[]{:S(2)}, u32[]{:S(2)}) collective-permute-start(f32[1,128]{1,0:T(1,128)S(1)} %add.38), channel_id=1, source_target_pairs={{0,128},{64,192},{128,0},{192,64},{1,129},{65,193},{129,1},{193,65... | collective-permute-start | bytes 1544 | tf_op jit(solution)/shard_map/ppermute | solution.py:398
